TPU v7x, 128 devices: a whole 4x4x4 slice. The times are simulated.
128 devices in a mesh: slab: 32 (over y, x, core), probe: 4 (over z).
Axes of the slice: x: 4, y: 4, z: 4, core: 2. Of those that a mesh axis runs over, the one named last changes fastest.
Arguments:
- probe_fields: bfloat16 [256, 128, 8192], P('probe', 'slab'), may hold values from -6 to 6
- sensor_rows: int32 [4096], replicated, may hold values from 0 to 126, as said below
- sensor_cols: int32 [4096], replicated, may hold values from 0 to 8190
- row_frac: float32 [4096], replicated, may hold values from 0 to 1
- col_frac: float32 [4096], replicated, may hold values from 0 to 1
- sensor_weights: float32 [4096], replicated, may hold values from 0.05 to 1
- owner_order: int32 [4096], replicated, may hold values from 0 to 4095, as said below
Outputs:
- adjoint_sources: bfloat16 [256, 128, 8192], P('probe', 'slab')
- observed: float32 [256, 4096], P('probe', 'slab')
- trace_mean: float32 [], replicated
Inputs may be any that keep to these rules, and one draw needn't show every extreme that they name: `sensor_rows`: rows run from 0 to 126. The sensors whose row lies in one slab of 4 rows number at most 512, and some slab holds exactly 512. `owner_order`: A permutation. The 4096 // 32 slots of one owner name at most 16 sensors whose row lies in any one slab, and every owner reaches 16 for some slab.
All inputs are finite; a program needn't handle non-finite values.
Results may differ from a plain program's by a relative error of at most 0.0068.
Values sent between devices are 32-bit elements; how exact they have to be, the bound alone decides.
No kernel may reach another device: no remote copies, remote signals or barrier semaphores. Data moves between devices by JAX's collectives and lax.ppermute only.
A program may use at most 64 MiB of HBM per device.

v0:
```python
import jax
import jax.numpy as jnp
from jax import lax
from jax.sharding import Mesh
from jax.sharding import PartitionSpec as P

SLAB = ("slab_0", "slab_1", "slab_2")
SLAB_PROBE = ("slab_0", "slab_1", "slab_2", "probe")


def in_blocks(x, dim, length):
    before, after = (x.shape[:dim], x.shape[dim + 1 :])
    return jnp.moveaxis(x.reshape(*before, length, -1, *after), dim, 0)


def summed_on_arrival(x, axis, dim):
    pieces = in_blocks(x, dim, lax.axis_size(axis))
    arrived = lax.all_to_all(pieces, axis, split_axis=0, concat_axis=0, tiled=True)
    return arrived.sum(axis=0)


def by_axis(x, axes):
    for axis in axes:
        x = lax.psum(x, axis)
    return x


def in_order(pieces, dim):
    lengths = list(pieces.shape[1:])
    lengths[dim] *= pieces.shape[0]
    return jnp.moveaxis(pieces, 0, dim).reshape(lengths)


def from_everyone(x, axis):
    length = lax.axis_size(axis)
    return lax.all_to_all(jnp.broadcast_to(x[None], (length, *x.shape)), axis, 0, 0, tiled=True)


def gather_directly(x, axis, dim):
    return in_order(from_everyone(x, axis), dim)


def column_table(columns, fractions, start, count, across):
    low_value = (1.0 - fractions).astype(jnp.bfloat16)
    high_value = fractions.astype(jnp.bfloat16)
    zero_value = jnp.zeros((), jnp.bfloat16)
    if across:
        cells = start + lax.broadcasted_iota(jnp.int32, (columns.shape[0], count), 1)
        where_col = columns[:, None]
        low_b = low_value[:, None]
        high_b = high_value[:, None]
    else:
        cells = start + lax.broadcasted_iota(jnp.int32, (count, columns.shape[0]), 0)
        where_col = columns[None, :]
        low_b = low_value[None, :]
        high_b = high_value[None, :]
    return jnp.where(
        cells == where_col, low_b, jnp.where(cells == where_col + 1, high_b, zero_value)
    )


def adjoint_grid(sources, columns, fractions, width):
    column_block = min(1024, width)

    def adjoint_block(number, result):
        begin = number * column_block
        table = column_table(columns, fractions, begin, column_block, True)
        piece = jnp.dot(sources, table, preferred_element_type=jnp.float32)
        return lax.dynamic_update_slice_in_dim(result, piece.astype(jnp.bfloat16), begin, 1)

    return lax.fori_loop(
        0, width // column_block, adjoint_block, jnp.zeros((sources.shape[0], width), jnp.bfloat16)
    )


def body(probe_fields, sensor_rows, sensor_cols, row_frac, col_frac, sensor_weights, owner_order):
    probe_count, row_count, width = probe_fields.shape
    sensor_count = sensor_rows.shape[0]
    depth = probe_count * row_count
    owned_rows = sensor_rows[owner_order]
    owned_cols = sensor_cols[owner_order]
    owned_rowfrac = row_frac[owner_order]
    owned_colfrac = col_frac[owner_order]
    owned_weights = sensor_weights[owner_order]
    slab_index = lax.axis_index(SLAB)
    first_row = slab_index * row_count
    slab_count = lax.axis_size(SLAB)
    own_count = sensor_count // slab_count
    own_begin = slab_index * own_count
    total_count = probe_count * lax.axis_size("probe") * sensor_count
    local_rows = first_row + lax.broadcasted_iota(jnp.int32, (row_count, sensor_count), 0)
    row_weights = jnp.where(local_rows == owned_rows[None, :], 1.0 - owned_rowfrac[None, :], 0.0)
    row_weights = row_weights + jnp.where(
        local_rows == owned_rows[None, :] + 1, owned_rowfrac[None, :], 0.0
    )
    flat_fields = probe_fields.reshape(depth, width)
    sensor_block = min(512, sensor_count)

    def forward_block(number, partial_value):
        begin = number * sensor_block
        cols_block = lax.dynamic_slice_in_dim(owned_cols, begin, sensor_block)
        frac_block = lax.dynamic_slice_in_dim(owned_colfrac, begin, sensor_block)
        table = column_table(cols_block, frac_block, 0, width, False)
        along = jnp.dot(flat_fields, table, preferred_element_type=jnp.float32)
        along = along.reshape(probe_count, row_count, sensor_block)
        weights_block = lax.dynamic_slice_in_dim(row_weights, begin, sensor_block, 1)
        summed = jnp.sum(along * weights_block[None, :, :], axis=1)
        return lax.dynamic_update_slice_in_dim(partial_value, summed, begin, 1)

    partial_value = lax.fori_loop(
        0,
        sensor_count // sensor_block,
        forward_block,
        jnp.zeros((probe_count, sensor_count), jnp.float32),
    )
    observed = summed_on_arrival(partial_value, SLAB, 1)
    own_weights = lax.dynamic_slice_in_dim(owned_weights, own_begin, own_count)
    spread_own = observed * own_weights[None, :]
    total = by_axis(jnp.sum(spread_own * observed), SLAB_PROBE)
    spread = gather_directly(spread_own, SLAB, 1)
    sources = (spread[:, None, :] * row_weights[None, :, :]).astype(jnp.bfloat16)
    sources = sources.reshape(depth, sensor_count)
    result = adjoint_grid(sources, owned_cols, owned_colfrac, width)
    trace_mean = total / total_count
    adjoint_sources = result.reshape(probe_count, row_count, width)
    return (adjoint_sources, observed, trace_mean)


def solution(mesh):
    torus = Mesh(
        mesh.devices.reshape(4, 4, 2, mesh.shape["probe"]), ("slab_0", "slab_1", "slab_2", "probe")
    )
    placed = (P("probe", SLAB, None), P(), P(), P(), P(), P(), P())
    return jax.shard_map(
        body,
        mesh=torus,
        in_specs=placed,
        out_specs=(P("probe", SLAB, None), P("probe", SLAB), P()),
        check_vma=False,
    )
```

profile of v0, /device:TPU:1, one launch (start us, length us, event | category | flops | bytes accessed | tf_op | source)
XLA Modules:
  0.0 336.7 jit_solution(1207151873596464338)
XLA Ops:
  1.4 23.0 %gather_fusion.1 = f32[4096]{0:T(1024)S(1)} fusion(f32[4096]{0:T(1024)S(1)} %copy-done, s32[4096]{0:T(1024)S(1)} %fusion.23), kind=kCustom, calls=%fused_computation.1 | custom fusion | bytes 49152 | tf_op jit(solution)/shard_map/gather | solution.py:83
  24.5 23.0 %gather_fusion.3 = f32[4096]{0:T(1024)S(1)} fusion(f32[4096]{0:T(1024)S(1)} %copy-done.1, s32[4096]{0:T(1024)S(1)} %fusion.23), kind=kCustom, calls=%fused_computation.3 | custom fusion | bytes 49152 | tf_op jit(solution)/shard_map/gather | solution.py:82
  47.5 23.0 %gather_fusion.2 = s32[4096]{0:T(1024)S(1)} fusion(s32[4096]{0:T(1024)S(1)} %copy-done.2, s32[4096]{0:T(1024)S(1)} %fusion.23), kind=kCustom, calls=%fused_computation.2 | custom fusion | bytes 49152 | tf_op jit(solution)/shard_map/gather | solution.py:80
  70.6 23.0 %gather_fusion = s32[4096]{0:T(1024)S(1)} fusion(s32[4096]{0:T(1024)S(1)} %copy-done.3, s32[4096]{0:T(1024)S(1)} %fusion.23), kind=kCustom, calls=%fused_computation | custom fusion | bytes 49152 | tf_op jit(solution)/shard_map/gather | solution.py:81
  93.6 6.9 %reshape.166 = bf16[256,8192]{1,0:T(8,128)(2,1)} reshape(bf16[64,4,8192]{2,1,0:T(4,128)(2,1)} %param.11) | data formatting | bytes 8388608 | tf_op jit(solution)/shard_map/reshape | solution.py:96
  100.7 48.5 %while.28 = (s32[]{:T(128)}, f32[64,4096]{1,0:T(8,128)S(1)}, s32[4096]{0:T(1024)S(1)}, f32[4096]{0:T(1024)S(1)}, bf16[256,8192]{1,0:T(8,128)(2,1)}, /*index=5*/f...) while((s32[]{:T(128)}, f32[64,4096]{1,0:T(8,128)S(1)}, s32[4096]{0:T(1024)S(1)}, ...), condition=%wide.region_2.3_spmd, body=%wide.region_0.2_spmd.sunk | while | flops 2164491776 | bytes 6726823 | solution.py:110
  100.9 5.3 %fusion.34 = f32[256,512]{1,0:T(8,128)S(1)} fusion(bf16[256,8192]{1,0:T(8,128)(2,1)} %get-tuple-element.389, s32[512]{0:T(512)S(1)} %get-tuple-element.356, s32[512]{0:T(512)S(1)} %get-tuple-element.357, bf16[512]{0:T(512)(128)(2,1)S(1)} %dynamic_slice.37, bf16[512]{0:T(512)(128)(2,1)S(1)} %subtract_convert_fusion.4), kind=kOutput, calls=%fused_computation.14.clone.1 | convolution fusion | flops 2164260864 | bytes 4724736 | tf_op jit(solution)/shard_map/while/body/eval_jaxpr/dot_general | solution.py:104
  107.0 5.3 %fusion.34 = f32[256,512]{1,0:T(8,128)S(1)} fusion(bf16[256,8192]{1,0:T(8,128)(2,1)} %get-tuple-element.389, s32[512]{0:T(512)S(1)} %get-tuple-element.356, s32[512]{0:T(512)S(1)} %get-tuple-element.357, bf16[512]{0:T(512)(128)(2,1)S(1)} %dynamic_slice.37, bf16[512]{0:T(512)(128)(2,1)S(1)} %subtract_convert_fusion.4), kind=kOutput, calls=%fused_computation.14.clone.1 | convolution fusion | flops 2164260864 | bytes 4724736 | tf_op jit(solution)/shard_map/while/body/eval_jaxpr/dot_general | solution.py:104
  113.1 5.3 %fusion.34 = f32[256,512]{1,0:T(8,128)S(1)} fusion(bf16[256,8192]{1,0:T(8,128)(2,1)} %get-tuple-element.389, s32[512]{0:T(512)S(1)} %get-tuple-element.356, s32[512]{0:T(512)S(1)} %get-tuple-element.357, bf16[512]{0:T(512)(128)(2,1)S(1)} %dynamic_slice.37, bf16[512]{0:T(512)(128)(2,1)S(1)} %subtract_convert_fusion.4), kind=kOutput, calls=%fused_computation.14.clone.1 | convolution fusion | flops 2164260864 | bytes 4724736 | tf_op jit(solution)/shard_map/while/body/eval_jaxpr/dot_general | solution.py:104
  119.1 5.3 %fusion.34 = f32[256,512]{1,0:T(8,128)S(1)} fusion(bf16[256,8192]{1,0:T(8,128)(2,1)} %get-tuple-element.389, s32[512]{0:T(512)S(1)} %get-tuple-element.356, s32[512]{0:T(512)S(1)} %get-tuple-element.357, bf16[512]{0:T(512)(128)(2,1)S(1)} %dynamic_slice.37, bf16[512]{0:T(512)(128)(2,1)S(1)} %subtract_convert_fusion.4), kind=kOutput, calls=%fused_computation.14.clone.1 | convolution fusion | flops 2164260864 | bytes 4724736 | tf_op jit(solution)/shard_map/while/body/eval_jaxpr/dot_general | solution.py:104
  125.2 5.3 %fusion.34 = f32[256,512]{1,0:T(8,128)S(1)} fusion(bf16[256,8192]{1,0:T(8,128)(2,1)} %get-tuple-element.389, s32[512]{0:T(512)S(1)} %get-tuple-element.356, s32[512]{0:T(512)S(1)} %get-tuple-element.357, bf16[512]{0:T(512)(128)(2,1)S(1)} %dynamic_slice.37, bf16[512]{0:T(512)(128)(2,1)S(1)} %subtract_convert_fusion.4), kind=kOutput, calls=%fused_computation.14.clone.1 | convolution fusion | flops 2164260864 | bytes 4724736 | tf_op jit(solution)/shard_map/while/body/eval_jaxpr/dot_general | solution.py:104
  131.3 5.3 %fusion.34 = f32[256,512]{1,0:T(8,128)S(1)} fusion(bf16[256,8192]{1,0:T(8,128)(2,1)} %get-tuple-element.389, s32[512]{0:T(512)S(1)} %get-tuple-element.356, s32[512]{0:T(512)S(1)} %get-tuple-element.357, bf16[512]{0:T(512)(128)(2,1)S(1)} %dynamic_slice.37, bf16[512]{0:T(512)(128)(2,1)S(1)} %subtract_convert_fusion.4), kind=kOutput, calls=%fused_computation.14.clone.1 | convolution fusion | flops 2164260864 | bytes 4724736 | tf_op jit(solution)/shard_map/while/body/eval_jaxpr/dot_general | solution.py:104
  137.4 5.3 %fusion.34 = f32[256,512]{1,0:T(8,128)S(1)} fusion(bf16[256,8192]{1,0:T(8,128)(2,1)} %get-tuple-element.389, s32[512]{0:T(512)S(1)} %get-tuple-element.356, s32[512]{0:T(512)S(1)} %get-tuple-element.357, bf16[512]{0:T(512)(128)(2,1)S(1)} %dynamic_slice.37, bf16[512]{0:T(512)(128)(2,1)S(1)} %subtract_convert_fusion.4), kind=kOutput, calls=%fused_computation.14.clone.1 | convolution fusion | flops 2164260864 | bytes 4724736 | tf_op jit(solution)/shard_map/while/body/eval_jaxpr/dot_general | solution.py:104
  143.4 5.3 %fusion.34 = f32[256,512]{1,0:T(8,128)S(1)} fusion(bf16[256,8192]{1,0:T(8,128)(2,1)} %get-tuple-element.389, s32[512]{0:T(512)S(1)} %get-tuple-element.356, s32[512]{0:T(512)S(1)} %get-tuple-element.357, bf16[512]{0:T(512)(128)(2,1)S(1)} %dynamic_slice.37, bf16[512]{0:T(512)(128)(2,1)S(1)} %subtract_convert_fusion.4), kind=kOutput, calls=%fused_computation.14.clone.1 | convolution fusion | flops 2164260864 | bytes 4724736 | tf_op jit(solution)/shard_map/while/body/eval_jaxpr/dot_general | solution.py:104
  151.0 8.6 %all-to-all-start = ((f32[32,64,128]{2,1,0:T(8,128)}), f32[32,64,128]{2,1,0:T(8,128)S(1)}, u32[]{:S(2)}, u32[]{:S(2)}) async-start(f32[32,64,128]{2,1,0:T(8,128)} %copy.13), calls=%async_computation | async-start | bytes 2097152 | tf_op jit(solution)/shard_map/all_to_all | solution.py:18
  159.6 23.0 %gather_fusion.4 = f32[4096]{0:T(1024)S(1)} fusion(f32[4096]{0:T(1024)S(1)} %copy-done.4, s32[4096]{0:T(1024)S(1)} %fusion.23), kind=kCustom, calls=%fused_computation.4 | custom fusion | bytes 49152 | tf_op jit(solution)/shard_map/gather | solution.py:84
  184.5 7.4 %all-to-all-start.1 = ((f32[32,64,128]{2,1,0:T(8,128)}), f32[32,64,128]{2,1,0:T(8,128)S(1)}, u32[]{:S(2)}, u32[]{:S(2)}) async-start(f32[32,64,128]{2,1,0:T(8,128)} %broadcast_in_dim.161), calls=%async_computation.1 | async-start | bytes 2097152 | tf_op jit(solution)/shard_map/all_to_all | solution.py:36
  191.9 11.8 %psum.28 = f32[]{:T(128)} all-reduce(f32[]{:T(128)} %get-tuple-element.279), channel_id=1, replica_groups=mesh['slab_0'=4,'slab_1'=4,'slab_2'=2,'probe'=4] {'slab_0'}, use_global_device_ids=true, to_apply=%region_7.8 | all-reduce | flops 1 | bytes 8 | tf_op jit(solution)/shard_map/psum | solution.py:24
  203.7 12.4 %psum.29 = f32[]{:T(128)} all-reduce(f32[]{:T(128)} %psum.28), channel_id=1, replica_groups=mesh['slab_0'=4,'slab_1'=4,'slab_2'=2,'probe'=4] {'slab_1'}, use_global_device_ids=true, to_apply=%region_8.9 | all-reduce | flops 1 | bytes 8 | tf_op jit(solution)/shard_map/psum | solution.py:24
  216.1 7.5 %psum.30 = f32[]{:T(128)} all-reduce(f32[]{:T(128)} %psum.29), channel_id=1, replica_groups=mesh['slab_0'=4,'slab_1'=4,'slab_2'=2,'probe'=4] {'slab_2'}, use_global_device_ids=true, to_apply=%region_9.10 | all-reduce | flops 1 | bytes 8 | tf_op jit(solution)/shard_map/psum | solution.py:24
  223.7 10.6 %psum.31 = f32[]{:T(128)} all-reduce(f32[]{:T(128)} %psum.30), channel_id=1, replica_groups=mesh['slab_0'=4,'slab_1'=4,'slab_2'=2,'probe'=4] {'probe'}, use_global_device_ids=true, to_apply=%region_10.11 | all-reduce | flops 1 | bytes 8 | tf_op jit(solution)/shard_map/psum | solution.py:24
  235.0 2.4 broadcast_in_dim.155.clone
  237.4 91.1 %while.29 = (s32[]{:T(128)}, bf16[256,8192]{1,0:T(8,128)(2,1)}, s32[4096]{0:T(1024)S(1)}, f32[4096]{0:T(1024)S(1)}, bf16[4096,1]{0,1:T(2,128)(2,1)S(1)}, /*index...) while((s32[]{:T(128)}, bf16[256,8192]{1,0:T(8,128)(2,1)}, ...), condition=%wide.region_5.6_spmd.clone, body=%wide.region_4.5_spmd.clone.sunk | while | flops 2166633472 | bytes 12255405 | solution.py:71
  240.6 7.0 %fusion.36 = bf16[256,1024]{0,1:T(8,128)(2,1)S(1)} fusion(bf16[256,4096]{1,0:T(8,128)(2,1)} %convert_element_type.94, s32[1024]{0:T(1024)S(1)} %iota_add_fusion.3, s32[4096]{0:T(1024)S(1)} %broadcast_add_fusion.6, s32[4096]{0:T(1024)S(1)} %get-tuple-element.421, bf16[4096]{0:T(1024)(128)(2,1)S(1)} %reduce.2, ...), kind=kOutput, calls=%fused_computation.33.clone.1 | convolution fusion | flops 2164523008 | bytes 2674688 | tf_op jit(solution)/shard_map/while/body/eval_jaxpr/dot_general | solution.py:68
  252.1 7.0 %fusion.36 = bf16[256,1024]{0,1:T(8,128)(2,1)S(1)} fusion(bf16[256,4096]{1,0:T(8,128)(2,1)} %convert_element_type.94, s32[1024]{0:T(1024)S(1)} %iota_add_fusion.3, s32[4096]{0:T(1024)S(1)} %broadcast_add_fusion.6, s32[4096]{0:T(1024)S(1)} %get-tuple-element.421, bf16[4096]{0:T(1024)(128)(2,1)S(1)} %reduce.2, ...), kind=kOutput, calls=%fused_computation.33.clone.1 | convolution fusion | flops 2164523008 | bytes 2674688 | tf_op jit(solution)/shard_map/while/body/eval_jaxpr/dot_general | solution.py:68
  263.4 7.0 %fusion.36 = bf16[256,1024]{0,1:T(8,128)(2,1)S(1)} fusion(bf16[256,4096]{1,0:T(8,128)(2,1)} %convert_element_type.94, s32[1024]{0:T(1024)S(1)} %iota_add_fusion.3, s32[4096]{0:T(1024)S(1)} %broadcast_add_fusion.6, s32[4096]{0:T(1024)S(1)} %get-tuple-element.421, bf16[4096]{0:T(1024)(128)(2,1)S(1)} %reduce.2, ...), kind=kOutput, calls=%fused_computation.33.clone.1 | convolution fusion | flops 2164523008 | bytes 2674688 | tf_op jit(solution)/shard_map/while/body/eval_jaxpr/dot_general | solution.py:68
  274.8 7.0 %fusion.36 = bf16[256,1024]{0,1:T(8,128)(2,1)S(1)} fusion(bf16[256,4096]{1,0:T(8,128)(2,1)} %convert_element_type.94, s32[1024]{0:T(1024)S(1)} %iota_add_fusion.3, s32[4096]{0:T(1024)S(1)} %broadcast_add_fusion.6, s32[4096]{0:T(1024)S(1)} %get-tuple-element.421, bf16[4096]{0:T(1024)(128)(2,1)S(1)} %reduce.2, ...), kind=kOutput, calls=%fused_computation.33.clone.1 | convolution fusion | flops 2164523008 | bytes 2674688 | tf_op jit(solution)/shard_map/while/body/eval_jaxpr/dot_general | solution.py:68
  286.2 7.0 %fusion.36 = bf16[256,1024]{0,1:T(8,128)(2,1)S(1)} fusion(bf16[256,4096]{1,0:T(8,128)(2,1)} %convert_element_type.94, s32[1024]{0:T(1024)S(1)} %iota_add_fusion.3, s32[4096]{0:T(1024)S(1)} %broadcast_add_fusion.6, s32[4096]{0:T(1024)S(1)} %get-tuple-element.421, bf16[4096]{0:T(1024)(128)(2,1)S(1)} %reduce.2, ...), kind=kOutput, calls=%fused_computation.33.clone.1 | convolution fusion | flops 2164523008 | bytes 2674688 | tf_op jit(solution)/shard_map/while/body/eval_jaxpr/dot_general | solution.py:68
  297.6 7.0 %fusion.36 = bf16[256,1024]{0,1:T(8,128)(2,1)S(1)} fusion(bf16[256,4096]{1,0:T(8,128)(2,1)} %convert_element_type.94, s32[1024]{0:T(1024)S(1)} %iota_add_fusion.3, s32[4096]{0:T(1024)S(1)} %broadcast_add_fusion.6, s32[4096]{0:T(1024)S(1)} %get-tuple-element.421, bf16[4096]{0:T(1024)(128)(2,1)S(1)} %reduce.2, ...), kind=kOutput, calls=%fused_computation.33.clone.1 | convolution fusion | flops 2164523008 | bytes 2674688 | tf_op jit(solution)/shard_map/while/body/eval_jaxpr/dot_general | solution.py:68
  309.0 7.0 %fusion.36 = bf16[256,1024]{0,1:T(8,128)(2,1)S(1)} fusion(bf16[256,4096]{1,0:T(8,128)(2,1)} %convert_element_type.94, s32[1024]{0:T(1024)S(1)} %iota_add_fusion.3, s32[4096]{0:T(1024)S(1)} %broadcast_add_fusion.6, s32[4096]{0:T(1024)S(1)} %get-tuple-element.421, bf16[4096]{0:T(1024)(128)(2,1)S(1)} %reduce.2, ...), kind=kOutput, calls=%fused_computation.33.clone.1 | convolution fusion | flops 2164523008 | bytes 2674688 | tf_op jit(solution)/shard_map/while/body/eval_jaxpr/dot_general | solution.py:68
  320.4 7.0 %fusion.36 = bf16[256,1024]{0,1:T(8,128)(2,1)S(1)} fusion(bf16[256,4096]{1,0:T(8,128)(2,1)} %convert_element_type.94, s32[1024]{0:T(1024)S(1)} %iota_add_fusion.3, s32[4096]{0:T(1024)S(1)} %broadcast_add_fusion.6, s32[4096]{0:T(1024)S(1)} %get-tuple-element.421, bf16[4096]{0:T(1024)(128)(2,1)S(1)} %reduce.2, ...), kind=kOutput, calls=%fused_computation.33.clone.1 | convolution fusion | flops 2164523008 | bytes 2674688 | tf_op jit(solution)/shard_map/while/body/eval_jaxpr/dot_general | solution.py:68
  328.5 7.2 %reshape.168 = bf16[64,4,8192]{2,1,0:T(4,128)(2,1)} reshape(bf16[256,8192]{1,0:T(8,128)(2,1)} %get-tuple-element.232) | data formatting | bytes 8388608 | tf_op jit(solution)/shard_map/reshape | solution.py:125
  (149 shorter events, 45.1 us)
Async XLA Ops:
  0.6 0.8 copy-start
  1.4 23.1 %copy-start.1 = (f32[4096]{0:T(1024)S(1)}, f32[4096]{0:T(1024)}, u32[]{:S(2)}) copy-start(f32[4096]{0:T(1024)} %param.14) | copy-start | bytes 49156
  24.5 23.1 %copy-start.2 = (s32[4096]{0:T(1024)S(1)}, s32[4096]{0:T(1024)}, u32[]{:S(2)}) copy-start(s32[4096]{0:T(1024)} %param.12) | copy-start | bytes 49156
  47.5 23.1 %copy-start.3 = (s32[4096]{0:T(1024)S(1)}, s32[4096]{0:T(1024)}, u32[]{:S(2)}) copy-start(s32[4096]{0:T(1024)} %param.13) | copy-start | bytes 49156
  149.2 10.4 %copy-start.4 = (f32[4096]{0:T(1024)S(1)}, f32[4096]{0:T(1024)}, u32[]{:S(2)}) copy-start(f32[4096]{0:T(1024)} %param.16) | copy-start | bytes 49156
  151.0 31.7 %all-to-all-start = ((f32[32,64,128]{2,1,0:T(8,128)}), f32[32,64,128]{2,1,0:T(8,128)S(1)}, u32[]{:S(2)}, u32[]{:S(2)}) async-start(f32[32,64,128]{2,1,0:T(8,128)} %copy.13), calls=%async_computation | async-start | bytes 2097152 | tf_op jit(solution)/shard_map/all_to_all | solution.py:18
  182.8 54.5 %copy-start.5 = (f32[64,128]{1,0:T(8,128)}, f32[64,128]{1,0:T(8,128)S(1)}, u32[]{:S(2)}) copy-start(f32[64,128]{1,0:T(8,128)S(1)} %reduce_sum.31) | copy-start | bytes 98308
  184.5 50.3 %all-to-all-start.1 = ((f32[32,64,128]{2,1,0:T(8,128)}), f32[32,64,128]{2,1,0:T(8,128)S(1)}, u32[]{:S(2)}, u32[]{:S(2)}) async-start(f32[32,64,128]{2,1,0:T(8,128)} %broadcast_in_dim.161), calls=%async_computation.1 | async-start | bytes 2097152 | tf_op jit(solution)/shard_map/all_to_all | solution.py:36
where the time goes:
time: 339 us; the launch traced here: 337 us
  local copies, waits for them, and re-layouts  161 us (47%)
  matrix products  98.4 us (29%)
  blocking collectives  42.3 us (12%)
  starting transfers between devices  16 us (5%)
  other arithmetic  15.2 us (4%)
    dot_general x8, matrix products, adjoint_block(): piece = jnp.dot(sources, table, preferred_element_type=jnp.float32)  56.2 us
    psum x4, blocking collectives, by_axis(): x = lax.psum(x, axis)  42.3 us
    dot_general x8, matrix products, forward_block(): along = jnp.dot(flat_fields, table, preferred_element_type=jnp.float32)  42.2 us
    gather x1, local copies, waits for them, and re-layouts, body(): owned_colfrac = col_frac[owner_order]  23 us
    gather x1, local copies, waits for them, and re-layouts, body(): owned_rowfrac = row_frac[owner_order]  23 us
    gather x1, local copies, waits for them, and re-layouts, body(): owned_rows = sensor_rows[owner_order]  23 us
    gather x1, local copies, waits for them, and re-layouts, body(): owned_cols = sensor_cols[owner_order]  23 us
    gather x1, local copies, waits for them, and re-layouts, body(): owned_weights = sensor_weights[owner_order]  23 us
  transfers between devices with their start and end apart: 2, of which 0 were waited for; matrix products, arithmetic and copies ran while one was open for 7% of the time, Pallas kernels for 0%

commit v1 on v0

v1 whole, which is shorter than its diff:
```python
import jax
import jax.numpy as jnp
from jax import lax
from jax.experimental import pallas as pl
from jax.experimental.pallas import tpu as pltpu
from jax.sharding import PartitionSpec as P

F32 = jnp.float32
BF16 = jnp.bfloat16
LANES = 128
SLOTS = 16
VMEM_LIMIT = 60 * 2**20


def iota(shape, dim):
    return lax.broadcasted_iota(jnp.int32, shape, dim)


def one_hot(mask):
    return jnp.where(mask, 1.0, 0.0).astype(BF16)


def dot(a, b, dims=((1,), (0,))):
    return lax.dot_general(a, b, (dims, ((), ())), preferred_element_type=F32)


def pieces(x):
    high = x.astype(BF16)
    return high, (x - high.astype(F32)).astype(BF16)


def pieces3(x):
    high = x.astype(BF16)
    rest = x - high.astype(F32)
    mid = rest.astype(BF16)
    return high, mid, (rest - mid.astype(F32)).astype(BF16)


def lookup_rows(order_hi, order_lo, rows):
    out = jnp.zeros(rows.shape, jnp.int32)
    for h in range(rows.shape[0]):
        line = jnp.broadcast_to(rows[h : h + 1, :], rows.shape)
        got = jnp.take_along_axis(line, order_lo, axis=1, mode="promise_in_bounds")
        out = jnp.where(order_hi == h, got, out)
    return out


def slot_lists(slab, owned_rows, order_hi, order_lo, rows, cols, row_frac, col_frac, weights):
    owners = rows.shape[0]
    per_list = owners * SLOTS
    total = 2 * per_list
    upper = one_hot(iota((LANES, LANES), 0) < iota((LANES, LANES), 1))
    lane = iota((owners, per_list), 1)
    owner_of = (lane // 8) % owners == iota((owners, per_list), 0)
    picks = []
    for back in (0, 1):
        match = owned_rows // 4 == slab - back
        rank = dot(one_hot(match), upper)
        ranked = jnp.where(match, rank, -1.0).astype(BF16)
        spread_rank = dot(ranked, one_hot(owner_of), ((0,), (0,)))
        place = iota((1, per_list), 1)
        place = ((place // (8 * owners)) * 8 + place % 8).astype(F32)
        picks.append(jnp.where(spread_rank == place, 1.0, 0.0))
    pick = jnp.concatenate(picks, axis=1)
    present = jnp.sum(pick, axis=0, keepdims=True)
    pick = pick.astype(BF16)
    owner_mask = jnp.concatenate([jnp.where(owner_of, 1.0, 0.0)] * 2, axis=1)
    ids = jnp.concatenate([order_hi, order_lo], axis=0).astype(F32).astype(BF16)
    got = dot(ids, pick)
    id_hi = jnp.sum(got[:owners] * owner_mask, axis=0, keepdims=True)
    id_lo = jnp.sum(got[owners:] * owner_mask, axis=0, keepdims=True)
    lo_iota = iota((LANES, total), 0).astype(F32)
    low_pick = jnp.where(lo_iota == id_lo, present, 0.0).astype(BF16)
    hi_mask = jnp.where(iota((owners, total), 0).astype(F32) == id_hi, 1.0, 0.0)
    table = [rows.astype(F32).astype(BF16), (cols // LANES).astype(F32).astype(BF16), (cols % LANES).astype(F32).astype(BF16)]
    table += list(pieces(row_frac))
    table += [(1.0 - col_frac).astype(BF16), col_frac.astype(BF16)]
    table += list(pieces(weights))
    got = dot(jnp.concatenate(table, axis=0), low_pick)
    field = [jnp.sum(got[owners * n : owners * (n + 1)] * hi_mask, axis=0, keepdims=True) for n in range(len(table))]
    row, tile, inner, frac, clow, chigh, weight = (
        field[0], field[1], field[2], field[3] + field[4], field[5], field[6], field[7] + field[8],
    )
    local = (slab * 4).astype(F32)
    sides = []
    for r in range(4):
        here = local + r
        sides.append(jnp.where(row == here, 1.0 - frac, jnp.where(row + 1.0 == here, frac, 0.0)))
    return tile, inner, clow, chigh, sides, weight


def column_parts(inner, clow, chigh):
    count = inner.shape[1]
    cell = iota((LANES, count), 0).astype(F32)
    main = jnp.where(cell == inner, clow, jnp.where(cell == inner + 1.0, chigh, 0.0)).astype(BF16)
    first = iota((16, count), 0) == 0
    carry = jnp.where(first & (inner == LANES - 1.0), chigh, 0.0).astype(BF16)
    return main, carry


def column_table(number, tile, main, carry):
    one = jnp.ones((), BF16)
    zero = jnp.zeros((), BF16)
    is_tile = [jnp.where(tile == float(2 * number + k), one, zero) for k in (-1, 0, 1)]
    parts = []
    for k in (0, 1):
        parts.append(main[:16] * is_tile[k + 1] + carry * is_tile[k])
        for g in range(1, 8):
            parts.append(main[16 * g : 16 * g + 16] * is_tile[k + 1])
    return jnp.concatenate(parts, axis=0)


def sum_matrix():
    return one_hot(iota((64, 256), 0) == iota((64, 256), 1) // 4)


def forward_kernel(slab_ref, rows_ref, cols_ref, rf_ref, cf_ref, w_ref, order_ref, u_ref, part_ref, meta_ref, place_ref, scr, sem):
    chunks = 8
    width = scr.shape[1] // chunks

    def copy(c, k):
        where = pl.ds(c * width, width)
        return pltpu.make_async_copy(u_ref.at[:, k, where], scr.at[:, where, pl.ds(4 * k, 4)], sem.at[c, k])

    for c in range(chunks):
        for k in range(4):
            copy(c, k).start()
    slab = slab_ref[0]
    order = order_ref[...]
    order_hi = order // LANES
    order_lo = order % LANES
    rows = rows_ref[...]
    owned_rows = lookup_rows(order_hi, order_lo, rows)
    tile, inner, clow, chigh, sides, weight = slot_lists(
        slab, owned_rows, order_hi, order_lo, rows, cols_ref[...], rf_ref[...], cf_ref[...], w_ref[...]
    )
    zero = jnp.zeros_like(tile)
    meta_ref[...] = jnp.concatenate([tile, inner, clow, chigh] + sides + [weight] + [zero] * 7, axis=0)
    own = jnp.sum(jnp.where(iota(owned_rows.shape, 0) == slab, owned_rows // 4, 0).astype(F32), axis=0, keepdims=True)
    across = jnp.broadcast_to(own, (LANES, LANES))
    before = (across == across.T) & (iota((LANES, LANES), 0) < iota((LANES, LANES), 1))
    rank = jnp.sum(jnp.where(before, 1.0, 0.0), axis=0, keepdims=True)
    half = jnp.where(rank >= 8.0, 1.0, 0.0)
    place_ref[...] = jnp.concatenate([own * 8.0 + rank - 8.0 * half, half] + [jnp.zeros_like(own)] * 6, axis=0)
    main, carry = column_parts(inner, clow, chigh)
    tile16 = jnp.broadcast_to(tile, (16, tile.shape[1])).astype(BF16)
    total = tile.shape[1]
    acc = jnp.zeros((256, total), F32)
    for c in range(chunks):
        for k in range(4):
            copy(c, k).wait()
        for n in range(c * width // 2, (c + 1) * width // 2):
            fields = jnp.concatenate([scr[:, 2 * n].reshape(256, LANES), scr[:, 2 * n + 1].reshape(256, LANES)], axis=1)
            acc = acc + dot(fields, column_table(n, tile16, main, carry))
    side = jnp.concatenate(sides * 2, axis=0)
    weighted = acc * jnp.tile(side, (32, 1))
    high, low = pieces(weighted)
    gather = sum_matrix()
    part_ref[...] = dot(gather, high) + dot(gather, low)


def combine_kernel(part_ref, above_ref, below_ref, meta_ref, probe_ref, send_ref, src_ref):
    count = above_ref.shape[1]
    value = part_ref[:, :count] + above_ref[...]
    before = part_ref[:, count:] + below_ref[...]
    weight = meta_ref[8:9, :]
    spread = jnp.concatenate([value, before], axis=1) * weight
    squares = jnp.sum(spread[:, :count] * value, axis=0, keepdims=True)
    trace = jnp.sum(squares, axis=1, keepdims=True)
    probe = probe_ref[0]
    groups = 4
    send_ref[...] = jnp.broadcast_to(trace, send_ref.shape)
    half = count // 2
    stacked = jnp.concatenate([value[:, :half], value[:, half:]], axis=0)
    blocks = stacked.T
    for o in range(half // 8):
        send_ref[pl.ds(9 * (groups * o + probe), 8), :] = blocks[8 * o : 8 * o + 8]
    repeat = one_hot(iota((256, 64), 0) // 4 == iota((256, 64), 1))
    tall = dot(repeat, spread.astype(BF16))
    side = jnp.concatenate([meta_ref[4:8, :]] * 2, axis=0)
    src_ref[...] = (tall * jnp.tile(side, (32, 1))).astype(BF16)


def adjoint_kernel(src_ref, meta_ref, out_ref, scr, sem):
    chunks = 8
    width = scr.shape[1] // chunks

    def copy(c, k):
        where = pl.ds(c * width, width)
        return pltpu.make_async_copy(scr.at[:, where, pl.ds(4 * k, 4)], out_ref.at[:, k, where], sem.at[c, k])

    tile, inner, clow, chigh = (meta_ref[n : n + 1, :] for n in range(4))
    main, carry = column_parts(inner, clow, chigh)
    tile16 = jnp.broadcast_to(tile, (16, tile.shape[1])).astype(BF16)
    sources = src_ref[...]
    for c in range(chunks):
        for n in range(c * width // 2, (c + 1) * width // 2):
            cells = dot(sources, column_table(n, tile16, main, carry), ((1,), (1,))).astype(BF16)
            scr[:, 2 * n] = cells[:, :LANES].reshape(16, 16, LANES)
            scr[:, 2 * n + 1] = cells[:, LANES:].reshape(16, 16, LANES)
        for k in range(4):
            copy(c, k).start()
    for c in range(chunks):
        for k in range(4):
            copy(c, k).wait()


def finish_kernel(got_ref, place_ref, probe_ref, observed_ref, total_ref):
    probe = probe_ref[0]
    groups = 4
    values = jnp.concatenate([got_ref[pl.ds(9 * (groups * q + probe), 8), :] for q in range(32)], axis=0)
    pick = one_hot(iota((256, LANES), 0).astype(F32) == place_ref[0:1, :])
    found = sum(dot(part, pick, ((0,), (0,))) for part in pieces3(values))
    observed_ref[...] = jnp.where(place_ref[1:2, :] > 0.5, found[64:], found[:64])
    traces = got_ref[pl.ds(8, 128, stride=9), :]
    total_ref[...] = jnp.broadcast_to(jnp.sum(traces, axis=0, keepdims=True), (8, LANES))


def call(kernel, inputs, spaces, outs, scratch=(), out_spaces=None):
    vmem, smem, anywhere = pltpu.VMEM, pltpu.SMEM, pl.ANY
    kinds = {"v": vmem, "s": smem, "h": anywhere}
    return pl.pallas_call(
        kernel,
        in_specs=[pl.BlockSpec(memory_space=kinds[k]) for k in spaces],
        out_specs=[pl.BlockSpec(memory_space=kinds[k]) for k in out_spaces or "v" * len(outs)],
        out_shape=[jax.ShapeDtypeStruct(*o) for o in outs],
        scratch_shapes=list(scratch),
        compiler_params=pltpu.CompilerParams(vmem_limit_bytes=VMEM_LIMIT),
        name=kernel.__name__,
    )(*inputs)


def body(probe_fields, sensor_rows, sensor_cols, row_frac, col_frac, sensor_weights, owner_order):
    slab = lax.axis_index("slab").astype(jnp.int32).reshape(1)
    probe = lax.axis_index("probe").astype(jnp.int32).reshape(1)
    slabs = lax.axis_size("slab")
    devices = slabs * lax.axis_size("probe")
    per_list = slabs * SLOTS
    tiles = probe_fields.shape[2] // LANES
    fields = probe_fields.reshape(16, 4, 4, tiles, LANES).transpose(0, 1, 3, 2, 4)
    flat = [x.reshape(slabs, LANES) for x in (sensor_rows, sensor_cols, row_frac, col_frac, sensor_weights, owner_order)]
    part, meta, place = call(
        forward_kernel,
        [slab] + flat + [fields],
        "svvvvvvh",
        [((64, 2 * per_list), F32), ((16, 2 * per_list), F32), ((8, LANES), F32)],
        [pltpu.VMEM((16, tiles, 16, LANES), BF16), pltpu.SemaphoreType.DMA((8, 4))],
    )
    up = [(i, i + 1) for i in range(slabs - 1)]
    down = [(i + 1, i) for i in range(slabs - 1)]
    below = lax.ppermute(part[:, :per_list], "slab", up)
    above = lax.ppermute(part[:, per_list:], "slab", down)
    send, sources = call(
        combine_kernel,
        [part, above, below, meta, probe],
        "vvvvs",
        [((9 * devices, LANES), F32), ((256, 2 * per_list), BF16)],
    )
    got = lax.all_to_all(send.reshape(devices, 1, 9 * LANES), ("slab", "probe"), 0, 0, tiled=True)
    (out,) = call(
        adjoint_kernel,
        [sources, meta],
        "vv",
        [(fields.shape, BF16)],
        [pltpu.VMEM((16, tiles, 16, LANES), BF16), pltpu.SemaphoreType.DMA((8, 4))],
        "h",
    )
    observed, total = call(
        finish_kernel,
        [got.reshape(9 * devices, LANES), place, probe],
        "vvs",
        [((64, LANES), F32), ((8, LANES), F32)],
    )
    adjoint = out.transpose(0, 1, 3, 2, 4).reshape(probe_fields.shape)
    count = probe_fields.shape[0] * lax.axis_size("probe") * sensor_rows.shape[0]
    return adjoint, observed, total[0, 0] / count


def solution(mesh):
    placed = (P("probe", "slab", None), P(), P(), P(), P(), P(), P())
    return jax.shard_map(
        body,
        mesh=mesh,
        in_specs=placed,
        out_specs=(P("probe", "slab", None), P("probe", "slab"), P()),
        check_vma=False,
    )
```

time: 339 us -> 56.2 us (0.17)
  local copies, waits for them, and re-layouts: 161 us -> 3.64 us
  matrix products: 98.4 us -> 0 us
  blocking collectives: 42.3 us -> 0 us
  Pallas kernels: 0 us -> 19.5 us
  other arithmetic: 15.2 us -> 0 us
  waiting for transfers between devices: 0.01 us -> 12.1 us
    gather x5 -> x0, local copies, waits for them, and re-layouts: 115 us -> none  [the longest x1 23 us: body(): owned_colfrac = col_frac[owner_order]]
    dot_general x16 -> x0, matrix products: 98.4 us -> none  [the longest x8 56.2 us: adjoint_block(): piece = jnp.dot(sources, table, preferred_element_type=jnp.float32)]
    psum x4 -> x0, blocking collectives: 42.3 us -> none  [by_axis(): x = lax.psum(x, axis)]
    pallas_call x0 -> x4, Pallas kernels: none -> 19.5 us  [call(): pl.pallas_call(kernel, in_specs=[pl.BlockSpec(memory_space=kinds[k]) for...]
    convert_element_type x9 -> x0, local copies, waits for them, and re-layouts: 16.2 us -> none  [the longest x8 16.1 us: body(): (spread[:, None, :] * row_weights[None, :, :]).astype(jnp.bfloat16)]
    reshape x10 -> x0, local copies, waits for them, and re-layouts: 15.2 us -> none  [the longest x1 7.16 us: body(): adjoint_sources = result.reshape(probe_count, row_count, width)]
    convert_element_type x25 -> x0, other arithmetic: 9.9 us -> none  [the longest x8 9.25 us: body(): (spread[:, None, :] * row_weights[None, :, :]).astype(jnp.bfloat16)]
    dynamic_update_slice x24 -> x0, local copies, waits for them, and re-layouts: 8.76 us -> none  [the longest x16 8.63 us: adjoint_block(): lax.dynamic_update_slice_in_dim(result, piece.astype(jnp.bfloat16), begin...]
  transfers between devices with their start and end apart: 2 -> 3, of which waited for: 0 -> 2; matrix products, arithmetic and copies ran while one was open for 7% -> 0% of each run, Pallas kernels for 0% -> 12%
where the time goes in v1:
time: 56.2 us; the launch traced here: 55.8 us
  Pallas kernels  19.5 us (35%)
  starting transfers between devices  18.1 us (32%)
  waiting for transfers between devices  12.1 us (22%)
  local copies, waits for them, and re-layouts  3.64 us (6%)
  between operations  2.48 us (4%)
    pallas_call x4, Pallas kernels, call(): pl.pallas_call(kernel, in_specs=[pl.BlockSpec(memory_space=kinds[k]) for...  19.5 us
    all_to_all x1, starting transfers between devices, body(): lax.all_to_all(send.reshape(devices, 1, 9 * LANES), ('slab', 'probe'), 0,...  11.7 us
    all_to_all x1, waiting for transfers between devices, body(): lax.all_to_all(send.reshape(devices, 1, 9 * LANES), ('slab', 'probe'), 0,...  7.78 us
    ppermute x1, starting transfers between devices, body(): below = lax.ppermute(part[:, :per_list], 'slab', up)  4.5 us
    ppermute x1, waiting for transfers between devices, body(): above = lax.ppermute(part[:, per_list:], 'slab', down)  4.34 us
    ppermute x1, starting transfers between devices, body(): above = lax.ppermute(part[:, per_list:], 'slab', down)  1.92 us
    unnamed x6, local copies, waits for them, and re-layouts  1.46 us
    slice x1, local copies, waits for them, and re-layouts, body(): return (adjoint, observed, total[0, 0] / count)  1.19 us
  transfers between devices with their start and end apart: 3, of which 2 were waited for; matrix products, arithmetic and copies ran while one was open for 0% of the time, Pallas kernels for 12%

profile of v1, /device:TPU:1, one launch (start us, length us, event | category | flops | bytes accessed | tf_op | source)
XLA Modules:
  0.0 55.8 jit_solution(2432591738800696611)
XLA Ops:
  0.6 8.6 %forward_kernel.1 = (f32[64,1024]{1,0:T(8,128)}, f32[16,1024]{1,0:T(8,128)}, f32[8,128]{1,0:T(8,128)}) custom-call(s32[1]{0:T(128)} %bitcast.slab_ref, s32[32,128]{1,0:T(8,128)} %bitcast.21, s32[32,128]{1,0:T(8,128)} %bitcast.22, f32[32,128]{1,0:T(8,128)} %bitcast.23, f32[32,128]{1,0:T(8,128)} %bitcast.24, f32[32,128]{1,0:T(8,128)} %bitcast.25, ...), custom_call_target="tpu_custom_call" | custom-call | tf_op jit(solution)/shard_map/forward_kernel/pallas_call | solution.py:222
  9.2 1.0 %fusion = (f32[64,512]{1,0:T(8,128)S(1)}, f32[64,512]{1,0:T(8,128)S(1)}) fusion(f32[64,1024]{1,0:T(8,128)} %get-tuple-element.10.part_ref), kind=kLoop, calls=%fused_computation | loop fusion | bytes 524288 | tf_op jit(solution)/shard_map/slice | solution.py:251
  10.2 4.5 %collective-permute-start.1 = (f32[64,512]{1,0:T(8,128)S(1)}, f32[64,512]{1,0:T(8,128)S(1)}, u32[]{:S(2)}, u32[]{:S(2)}) collective-permute-start(f32[64,512]{1,0:T(8,128)S(1)} %get-tuple-element.17), channel_id=1, source_target_pairs={{0,4},{4,8},{8,12},{12,16},{16,20},{20,24},{24,28},{28,32},{32,36}... | collective-permute-start | bytes 393224 | tf_op jit(solution)/shard_map/ppermute | solution.py:251
  14.7 1.9 %collective-permute-start = (f32[64,512]{1,0:T(8,128)S(1)}, f32[64,512]{1,0:T(8,128)S(1)}, u32[]{:S(2)}, u32[]{:S(2)}) collective-permute-start(f32[64,512]{1,0:T(8,128)S(1)} %get-tuple-element.18), channel_id=1, source_target_pairs={{4,0},{8,4},{12,8},{16,12},{20,16},{24,20},{28,24},{32,28},{36,32}... | collective-permute-start | bytes 393224 | tf_op jit(solution)/shard_map/ppermute | solution.py:252
  16.6 0.0 collective-permute-done.1.below_ref
  16.6 0.0 copy-start.1
  16.7 4.3 %collective-permute-done.above_ref = f32[64,512]{1,0:T(8,128)S(1)} collective-permute-done((f32[64,512]{1,0:T(8,128)S(1)}, f32[64,512]{1,0:T(8,128)S(1)}, u32[]{:S(2)}, u32[]{:S(2)}) %collective-permute-start) | collective-permute-done | bytes 131104 | tf_op jit(solution)/shard_map/ppermute | solution.py:252
  21.0 0.0 copy-start.2
  21.0 0.0 copy-done.1
  21.0 0.6 %copy-done.2 = f32[64,512]{1,0:T(8,128)} copy-done((f32[64,512]{1,0:T(8,128)}, f32[64,512]{1,0:T(8,128)S(1)}, u32[]{:S(2)}) %copy-start.2) | copy-done | bytes 131096
  21.6 2.3 %combine_kernel.1 = (f32[1152,128]{1,0:T(8,128)}, bf16[256,1024]{1,0:T(8,128)(2,1)}) custom-call(f32[64,1024]{1,0:T(8,128)} %get-tuple-element.10.part_ref, f32[64,512]{1,0:T(8,128)} %copy-done.2, f32[64,512]{1,0:T(8,128)} %copy-done.1, f32[16,1024]{1,0:T(8,128)} %get-tuple-element.11.meta_ref, s32[1]{0:T(128)} %bitcast.9.probe_ref), custom_call_target="tpu_custom_call" | custom-call | tf_op jit(solution)/shard_map/combine_kernel/pallas_call | solution.py:222
  23.9 11.7 %all-to-all-start = ((f32[128,1,1152]{2,1,0:T(1,128)}), f32[128,1,1152]{2,1,0:T(1,128)S(1)}, u32[]{:S(2)}, u32[]{:S(2)}) async-start(f32[128,1,1152]{2,1,0:T(1,128)} %bitcast.20), calls=%async_computation | async-start | bytes 1179648 | tf_op jit(solution)/shard_map/all_to_all | solution.py:259
  35.6 6.7 %adjoint_kernel.1 = bf16[16,4,64,4,128]{4,3,2,1,0:T(4,128)(2,1)} custom-call(bf16[256,1024]{1,0:T(8,128)(2,1)} %get-tuple-element.12.src_ref, f32[16,1024]{1,0:T(8,128)} %get-tuple-element.11.meta_ref), custom_call_target="tpu_custom_call" | custom-call | tf_op jit(solution)/shard_map/adjoint_kernel/pallas_call | solution.py:222
  42.3 7.8 %all-to-all-done = f32[128,1,1152]{2,1,0:T(1,128)S(1)} async-done(((f32[128,1,1152]{2,1,0:T(1,128)}), f32[128,1,1152]{2,1,0:T(1,128)S(1)}, u32[]{:S(2)}, u32[]{:S(2)}) %all-to-all-start) | async-done | bytes 589856 | tf_op jit(solution)/shard_map/all_to_all | solution.py:259
  50.1 0.0 copy-start
  50.1 0.8 %copy-done = f32[128,1,1152]{2,1,0:T(1,128)} copy-done((f32[128,1,1152]{2,1,0:T(1,128)}, f32[128,1,1152]{2,1,0:T(1,128)S(1)}, u32[]{:S(2)}) %copy-start) | copy-done | bytes 589848
  50.9 1.9 %finish_kernel.1 = (f32[64,128]{1,0:T(8,128)}, f32[8,128]{1,0:T(8,128)}) custom-call(f32[1152,128]{1,0:T(8,128)} %bitcast.19, f32[8,128]{1,0:T(8,128)} %get-tuple-element.14.place_ref, s32[1]{0:T(128)} %bitcast.9.probe_ref), custom_call_target="tpu_custom_call" | custom-call | tf_op jit(solution)/shard_map/finish_kernel/pallas_call | solution.py:222
  52.8 1.2 %slice.11 = f32[1,1]{1,0:T(1,128)} slice(f32[8,128]{1,0:T(8,128)} %get-tuple-element.16), slice={[0:1], [0:1]} | slice | bytes 8 | tf_op jit(solution)/shard_map/slice | solution.py:276
Async XLA Ops:
  10.2 6.4 %collective-permute-start.1 = (f32[64,512]{1,0:T(8,128)S(1)}, f32[64,512]{1,0:T(8,128)S(1)}, u32[]{:S(2)}, u32[]{:S(2)}) collective-permute-start(f32[64,512]{1,0:T(8,128)S(1)} %get-tuple-element.17), channel_id=1, source_target_pairs={{0,4},{4,8},{8,12},{12,16},{16,20},{20,24},{24,28},{28,32},{32,36}... | collective-permute-start | bytes 393224 | tf_op jit(solution)/shard_map/ppermute | solution.py:251
  14.7 6.3 %collective-permute-start = (f32[64,512]{1,0:T(8,128)S(1)}, f32[64,512]{1,0:T(8,128)S(1)}, u32[]{:S(2)}, u32[]{:S(2)}) collective-permute-start(f32[64,512]{1,0:T(8,128)S(1)} %get-tuple-element.18), channel_id=1, source_target_pairs={{4,0},{8,4},{12,8},{16,12},{20,16},{24,20},{28,24},{32,28},{36,32}... | collective-permute-start | bytes 393224 | tf_op jit(solution)/shard_map/ppermute | solution.py:252
  16.6 4.4 %copy-start.1 = (f32[64,512]{1,0:T(8,128)}, f32[64,512]{1,0:T(8,128)S(1)}, u32[]{:S(2)}) copy-start(f32[64,512]{1,0:T(8,128)S(1)} %collective-permute-done.1.below_ref) | copy-start | bytes 393220
  21.0 0.7 %copy-start.2 = (f32[64,512]{1,0:T(8,128)}, f32[64,512]{1,0:T(8,128)S(1)}, u32[]{:S(2)}) copy-start(f32[64,512]{1,0:T(8,128)S(1)} %collective-permute-done.above_ref) | copy-start | bytes 393220
  23.9 26.1 %all-to-all-start = ((f32[128,1,1152]{2,1,0:T(1,128)}), f32[128,1,1152]{2,1,0:T(1,128)S(1)}, u32[]{:S(2)}, u32[]{:S(2)}) async-start(f32[128,1,1152]{2,1,0:T(1,128)} %bitcast.20), calls=%async_computation | async-start | bytes 1179648 | tf_op jit(solution)/shard_map/all_to_all | solution.py:259
  50.1 0.8 %copy-start = (f32[128,1,1152]{2,1,0:T(1,128)}, f32[128,1,1152]{2,1,0:T(1,128)S(1)}, u32[]{:S(2)}) copy-start(f32[128,1,1152]{2,1,0:T(1,128)S(1)} %all-to-all-done) | copy-start | bytes 1769476

commit v2 on v1

v2 whole, which is shorter than its diff:
```python
import functools

import jax
import jax.numpy as jnp
from jax import lax
from jax.experimental import pallas as pl
from jax.experimental.pallas import tpu as pltpu
from jax.sharding import PartitionSpec as P

F32 = jnp.float32
BF16 = jnp.bfloat16
LANES = 128
SLOTS = 16
VMEM_LIMIT = 60 * 2**20
CHUNKS = 1
OUT_CHUNKS = 8


def iota(shape, dim):
    return lax.broadcasted_iota(jnp.int32, shape, dim)


def one_hot(mask):
    return jnp.where(mask, 1.0, 0.0).astype(BF16)


def dot(a, b, dims=((1,), (0,))):
    return lax.dot_general(a, b, (dims, ((), ())), preferred_element_type=F32)


def pieces(x):
    high = x.astype(BF16)
    return high, (x - high.astype(F32)).astype(BF16)


def pieces3(x):
    high = x.astype(BF16)
    rest = x - high.astype(F32)
    mid = rest.astype(BF16)
    return high, mid, (rest - mid.astype(F32)).astype(BF16)


def lookup_rows(order_hi, order_lo, rows):
    out = jnp.zeros(rows.shape, jnp.int32)
    for h in range(rows.shape[0]):
        line = jnp.broadcast_to(rows[h : h + 1, :], rows.shape)
        got = jnp.take_along_axis(line, order_lo, axis=1, mode="promise_in_bounds")
        out = jnp.where(order_hi == h, got, out)
    return out


def owner_slots(slab, owned_rows):
    upper = one_hot(iota((LANES, LANES), 0) < iota((LANES, LANES), 1))
    match = owned_rows // 4 == slab
    last = match & (owned_rows % 4 == 3)
    rank = dot(one_hot(match & ~last), upper)
    back_rank = dot(one_hot(last), upper)
    many = jnp.max(jnp.where(last & (back_rank > 7.5), 1.0, 0.0))
    return jnp.where(last, SLOTS - 1.0 - back_rank, jnp.where(match, rank, -1.0)).astype(BF16), many


def slot_fields(slab, slots, pieces_of, order_hi, order_lo, rows, cols, row_frac, col_frac, weights):
    owners = rows.shape[0]
    part = owners * 8
    lanes = iota((owners, part), 1)
    owner_of = one_hot((lanes // 8) % owners == iota((owners, part), 0))
    spread = [dot(x, owner_of, ((0,), (0,))) for x in slots]
    place = (iota((1, part), 1) % 8).astype(F32)
    pick = jnp.concatenate([jnp.where(spread[q] == place + 8.0 * half, 1.0, 0.0) for q, half in pieces_of], axis=1)
    present = jnp.sum(pick, axis=0, keepdims=True)
    total = pick.shape[1]
    owner_mask = jnp.concatenate([owner_of.astype(F32)] * len(pieces_of), axis=1)
    ids = jnp.concatenate([order_hi, order_lo], axis=0).astype(F32).astype(BF16)
    got = dot(ids, pick.astype(BF16))
    id_hi = jnp.sum(got[:owners] * owner_mask, axis=0, keepdims=True)
    id_lo = jnp.sum(got[owners:] * owner_mask, axis=0, keepdims=True)
    lo_iota = iota((LANES, total), 0).astype(F32)
    low_pick = jnp.where(lo_iota == id_lo, present, 0.0).astype(BF16)
    hi_mask = jnp.where(iota((owners, total), 0).astype(F32) == id_hi, 1.0, 0.0)
    table = [rows.astype(F32).astype(BF16), (cols // LANES).astype(F32).astype(BF16), (cols % LANES).astype(F32).astype(BF16)]
    table += list(pieces(row_frac))
    table += [(1.0 - col_frac).astype(BF16), col_frac.astype(BF16)]
    table += list(pieces(weights))
    got = dot(jnp.concatenate(table, axis=0), low_pick)
    field = [jnp.sum(got[owners * n : owners * (n + 1)] * hi_mask, axis=0, keepdims=True) for n in range(len(table))]
    row, tile, inner, frac, clow, chigh, weight = (
        field[0], field[1], field[2], field[3] + field[4], field[5], field[6], field[7] + field[8],
    )
    local = (slab * 4).astype(F32)
    sides = []
    for r in range(4):
        here = local + r
        sides.append(jnp.where(row == here, 1.0 - frac, jnp.where(row + 1.0 == here, frac, 0.0)))
    return jnp.concatenate([tile, inner, clow, chigh] + sides + [weight] + [jnp.zeros_like(tile)] * 7, axis=0)


def column_parts(meta):
    tile, inner, clow, chigh = (meta[n : n + 1] for n in range(4))
    count = inner.shape[1]
    cell = iota((LANES, count), 0).astype(F32)
    main = jnp.where(cell == inner, clow, jnp.where(cell == inner + 1.0, chigh, 0.0)).astype(BF16)
    first = iota((16, count), 0) == 0
    carry = jnp.where(first & (inner == LANES - 1.0), chigh, 0.0).astype(BF16)
    return main, carry, jnp.broadcast_to(tile, (16, count)).astype(BF16)


def row_sides(meta):
    return jnp.tile(jnp.concatenate([meta[4:8]] * 2, axis=0), (32, 1))


def column_table(number, tile, main, carry):
    one = jnp.ones((), BF16)
    zero = jnp.zeros((), BF16)
    first = 2.0 * number if isinstance(number, int) else 2.0 * number.astype(F32)
    is_tile = [jnp.where(tile == first + k, 1.0, 0.0).astype(BF16) if tile.dtype == F32 else jnp.where(tile == first + k, one, zero) for k in (-1, 0, 1)]
    parts = []
    for k in (0, 1):
        parts.append(main[:16] * is_tile[k + 1] + carry * is_tile[k])
        for g in range(1, 8):
            parts.append(main[16 * g : 16 * g + 16] * is_tile[k + 1])
    return jnp.concatenate(parts, axis=0)


def row_sum(x, group):
    count = x.shape[0] // group
    gather = one_hot(iota((count, x.shape[0]), 0) == iota((count, x.shape[0]), 1) // group)
    high, low = pieces(x)
    return dot(gather, high) + dot(gather, low)


def to_blocks(value):
    half = value.shape[1] // 2
    return jnp.concatenate([value[:, :half], value[:, half:]], axis=0).T


def field_block(scr, n):
    return jnp.concatenate([scr[:, 2 * n + m].reshape(256, LANES) for m in (0, 1)], axis=1)


def forward_kernel(
    slab_ref, rows_hbm, cols_hbm, rf_hbm, cf_hbm, w_hbm, order_hbm, u_ref,
    own_ref, last_ref, same_ref, cross_ref, meta_ref, place_ref, flag_ref,
    scr, small_i, small_f, sem, small_sem,
):
    chunks = CHUNKS
    width = scr.shape[1] // chunks

    def copy(c, k):
        where = pl.ds(c * width, width)
        return pltpu.make_async_copy(u_ref.at[:, k, where], scr.at[:, where, pl.ds(4 * k, 4)], sem.at[c, k])

    small = [
        pltpu.make_async_copy(src, dst, small_sem.at[n])
        for n, (src, dst) in enumerate(
            [(order_hbm, small_i.at[0]), (rows_hbm, small_i.at[1]), (cols_hbm, small_i.at[2])]
            + [(rf_hbm, small_f.at[0]), (cf_hbm, small_f.at[1]), (w_hbm, small_f.at[2])]
        )
    ]
    for x in small:
        x.start()
    for c in range(chunks):
        for k in range(4):
            copy(c, k).start()
    for x in small:
        x.wait()
    slab = slab_ref[0]
    order = small_i[0]
    order_hi = order // LANES
    order_lo = order % LANES
    rows = small_i[1]
    owned_rows = lookup_rows(order_hi, order_lo, rows)
    count = own_ref.shape[1]
    skip = count // 2
    given = (order_hi, order_lo, rows, small_i[2], small_f[0], small_f[1], small_f[2])
    own_slots, _ = owner_slots(slab, owned_rows)
    last_slots, many = owner_slots(slab - 1, owned_rows)
    flag_ref[0] = (many > 0.5).astype(jnp.int32)
    meta = slot_fields(slab, (own_slots, last_slots), ((0, 0), (0, 1), (1, 1)), *given)
    meta_ref[:, :count] = meta[:, :count]
    meta_ref[:, count : count + skip] = jnp.zeros((16, skip), F32)
    meta_ref[:, count + skip :] = meta[:, count:]
    own_rows = jnp.sum(jnp.where(iota(owned_rows.shape, 0) == slab, owned_rows, 0).astype(F32), axis=0, keepdims=True)
    own = jnp.floor(own_rows * 0.25)
    on_last = jnp.where(own_rows - own * 4.0 == 3.0, 1.0, 0.0)
    kind = jnp.broadcast_to(own * 2.0 + on_last, (LANES, LANES))
    before = (kind == kind.T) & (iota((LANES, LANES), 0) < iota((LANES, LANES), 1))
    rank = jnp.sum(jnp.where(before, 1.0, 0.0), axis=0, keepdims=True)
    rank = jnp.where(on_last > 0.5, SLOTS - 1.0 - rank, rank)
    half = jnp.where(rank >= 8.0, 1.0, 0.0)
    place_ref[...] = jnp.concatenate([own * 8.0 + rank - 8.0 * half, half] + [jnp.zeros_like(own)] * 6, axis=0)
    main, carry, tile16 = column_parts(meta)
    sums = [jnp.zeros((256, count), F32)] + [jnp.zeros((128, skip), F32)] * 2
    for c in range(chunks):
        for k in range(4):
            copy(c, k).wait()
        for n in range(c * width // 2, (c + 1) * width // 2):
            block = field_block(scr, n)
            table = column_table(n, tile16, main, carry)
            sums[0] = sums[0] + dot(block, table[:, :count])
            for m in (0, 1):
                sums[1 + m] = sums[1 + m] + dot(block[128 * m : 128 * m + 128], table[:, count:])
    acc = jnp.concatenate([sums[0], jnp.concatenate(sums[1:], axis=0)], axis=1)
    part = row_sum(acc * row_sides(meta), 4)
    even = slab % 2 == 0

    def give(own_part, last_part):
        last_ref[...] = last_part
        same_ref[...] = jnp.where(even, own_part, last_part)
        cross_ref[...] = jnp.where(even, last_part, own_part)

    own_ref[...] = part[:, :count]
    give(part[:, :count], jnp.concatenate([jnp.zeros((64, skip), F32), part[:, count:]], axis=1))

    @pl.when(flag_ref[0] != 0)
    def _():
        order = small_i[0]
        order_hi = order // LANES
        order_lo = order % LANES
        rows = small_i[1]
        slots, _ = owner_slots(slab - 1, lookup_rows(order_hi, order_lo, rows))
        given = (order_hi, order_lo, rows, small_i[2], small_f[0], small_f[1], small_f[2])
        far_meta = slot_fields(slab, (slots,), ((0, 0),), *given)
        meta_ref[:, count : count + skip] = far_meta
        far_main, far_carry, _ = column_parts(far_meta)
        far_tile = jnp.broadcast_to(far_meta[:1], (16, skip))

        def step(n, far):
            return far + dot(field_block(scr, n), column_table(n, far_tile, far_main, far_carry))

        far = lax.fori_loop(0, scr.shape[1] // 2, step, jnp.zeros((256, skip), F32))
        give(own_ref[...], jnp.concatenate([row_sum(far * row_sides(far_meta), 4), last_ref[:, skip:]], axis=1))


def combine_kernel(own_ref, last_ref, same_ref, cross_ref, meta_ref, at_ref, block_ref, trace_ref, src_ref):
    count = own_ref.shape[1]
    even = at_ref[0] % 2 == 0
    same = same_ref[...]
    cross = cross_ref[...]
    value = own_ref[...] + jnp.where(even, same, cross)
    before = last_ref[...] + jnp.where(even, cross, same)
    weight = meta_ref[8:9, :]
    spread = jnp.concatenate([value, before], axis=1) * weight
    squares = jnp.sum(spread[:, :count] * value, axis=0, keepdims=True)
    trace = jnp.sum(squares, axis=1, keepdims=True)
    lines = to_blocks(value)
    block_ref[...] = lines
    trace_ref[...] = jnp.broadcast_to(trace, trace_ref.shape)
    repeat = one_hot(iota((256, 64), 0) // 4 == iota((256, 64), 1))
    tall = dot(repeat, spread.astype(BF16))
    src_ref[...] = (tall * row_sides(meta_ref[...])).astype(BF16)


def adjoint_kernel(src_ref, meta_ref, flag_ref, out_ref, scr, sem):
    chunks = OUT_CHUNKS
    width = scr.shape[1] // chunks

    def copy(c, k):
        return pltpu.make_async_copy(
            scr.at[:, pl.ds(c * width, width), pl.ds(4 * k, 4)], out_ref.at[:, k, pl.ds(c * width, width)], sem.at[c, k]
        )

    def spread_all(keep):
        main, carry, tile16 = column_parts(keep(meta_ref[...]))
        sources = keep(src_ref[...])
        for c in range(chunks):
            for n in range(c * width // 2, (c + 1) * width // 2):
                table = column_table(n, tile16, main, carry)
                cells = dot(sources, table, ((1,), (1,))).astype(BF16)
                scr[:, 2 * n] = cells[:, :LANES].reshape(16, 16, LANES)
                scr[:, 2 * n + 1] = cells[:, LANES:].reshape(16, 16, LANES)
            for k in range(4):
                copy(c, k).start()

    count = meta_ref.shape[1] // 2

    @pl.when(flag_ref[0] == 0)
    def _():
        spread_all(lambda x: jnp.concatenate([x[:, :count], x[:, count + count // 2 :]], axis=1))

    @pl.when(flag_ref[0] != 0)
    def _():
        spread_all(lambda x: x)

    for c in range(chunks):
        for k in range(4):
            copy(c, k).wait()


def pack_kernel(block_ref, *refs):
    *trace_refs, send_ref = refs
    trace = sum(ref[...] for ref in trace_refs)[:1, :]
    for o in range(block_ref.shape[0] // 8):
        send_ref[9 * o : 9 * o + 8, :] = block_ref[8 * o : 8 * o + 8, :]
        send_ref[9 * o + 8 : 9 * o + 9, :] = trace


def finish_kernel(got_ref, place_ref, observed_ref, total_ref, *, scale):
    slabs = got_ref.shape[0] // 9
    values = jnp.concatenate([got_ref[9 * q : 9 * q + 8, :] for q in range(slabs)], axis=0)
    pick = one_hot(iota((8 * slabs, LANES), 0).astype(F32) == place_ref[0:1, :])
    found = sum(dot(part, pick, ((0,), (0,))) for part in pieces3(values))
    observed_ref[...] = jnp.where(place_ref[1:2, :] > 0.5, found[64:], found[:64])
    traces = jnp.sum(got_ref[pl.ds(8, slabs, stride=9), :], axis=0, keepdims=True)
    total_ref[...] = traces[:, :1] * scale


def call(kernel, inputs, outs, scratch=(), **params):
    kinds = {"v": pltpu.VMEM, "s": pltpu.SMEM, "h": pl.ANY, "w": pltpu.VMEM}
    arrays = [pltpu.with_memory_space_constraint(x, pltpu.VMEM) if k == "w" else x for k, x in inputs]
    return pl.pallas_call(
        functools.partial(kernel, **params),
        in_specs=[pl.BlockSpec(memory_space=kinds[k]) for k, _ in inputs],
        out_specs=[pl.BlockSpec(memory_space=kinds[k]) for k, _, _ in outs],
        out_shape=[pltpu.VMEM(s, t) if k == "w" else jax.ShapeDtypeStruct(s, t) for k, s, t in outs],
        scratch_shapes=list(scratch),
        compiler_params=pltpu.CompilerParams(vmem_limit_bytes=VMEM_LIMIT),
    )(*arrays)


def body(probe_fields, sensor_rows, sensor_cols, row_frac, col_frac, sensor_weights, owner_order):
    at = lax.axis_index("slab").astype(jnp.int32).reshape(1)
    slabs = lax.axis_size("slab")
    groups = lax.axis_size("probe")
    per_list = slabs * SLOTS
    tiles = probe_fields.shape[2] // LANES
    fields = probe_fields.reshape(16, 4, 4, tiles, LANES).transpose(0, 1, 3, 2, 4)
    flat = [x.reshape(slabs, LANES) for x in (sensor_rows, sensor_cols, row_frac, col_frac, sensor_weights, owner_order)]
    own, last, to_same, to_cross, meta, place, flag = call(
        forward_kernel,
        [("s", at)] + [("h", x) for x in flat] + [("h", fields)],
        [("w", (64, per_list), F32)] * 4
        + [("w", (16, 2 * per_list), F32), ("w", (8, LANES), F32), ("s", (1,), jnp.int32)],
        [
            pltpu.VMEM((16, tiles, 16, LANES), BF16),
            pltpu.VMEM((3, slabs, LANES), jnp.int32),
            pltpu.VMEM((3, slabs, LANES), F32),
            pltpu.SemaphoreType.DMA((CHUNKS, 4)),
            pltpu.SemaphoreType.DMA((6,)),
        ],
    )
    swap_cross = [(i, i + 1 if i % 2 else i - 1) for i in range(1, slabs - 1)]
    swap_same = [(i, i - 1 if i % 2 else i + 1) for i in range(slabs)]
    cross = lax.ppermute(to_cross, "slab", swap_cross)
    same = lax.ppermute(to_same, "slab", swap_same)
    blocks, trace, sources = call(
        combine_kernel,
        [("w", own), ("w", last), ("w", same), ("w", cross), ("w", meta), ("s", at)],
        [("w", (8 * slabs, LANES), F32), ("w", (8, LANES), F32), ("w", (256, 2 * per_list), BF16)],
    )
    traces = [trace]
    for k in range(1, groups):
        traces.append(lax.ppermute(trace, "probe", [(i, (i + k) % groups) for i in range(groups)]))
    (send,) = call(pack_kernel, [("w", blocks)] + [("w", x) for x in traces], [("w", (9 * slabs, LANES), F32)])
    got = lax.all_to_all(send.reshape(slabs, 1, 9 * LANES), "slab", 0, 0, tiled=True)
    (out,) = call(
        adjoint_kernel,
        [("w", sources), ("w", meta), ("s", flag)],
        [("h", fields.shape, BF16)],
        [pltpu.VMEM((16, tiles, 16, LANES), BF16), pltpu.SemaphoreType.DMA((OUT_CHUNKS, 4))],
    )
    count = probe_fields.shape[0] * groups * sensor_rows.shape[0]
    observed, total = call(
        finish_kernel,
        [("w", got.reshape(9 * slabs, LANES)), ("w", place)],
        [("v", (64, LANES), F32), ("v", (1, 1), F32)],
        scale=1.0 / count,
    )
    adjoint = out.transpose(0, 1, 3, 2, 4).reshape(probe_fields.shape)
    return adjoint, observed, total.reshape(())


def solution(mesh):
    placed = (P("probe", "slab", None), P(), P(), P(), P(), P(), P())

    return jax.shard_map(
        body,
        mesh=mesh,
        in_specs=placed,
        out_specs=(P("probe", "slab", None), P("probe", "slab"), P()),
        check_vma=False,
    )
```

time: 56.2 us -> 48.2 us (0.86)
  starting transfers between devices: 18.1 us -> 24.7 us
  Pallas kernels: 19.5 us -> 13.6 us
  local copies, waits for them, and re-layouts: 3.64 us -> 0 us
  waiting for transfers between devices: 12.1 us -> 8.95 us
  between operations: 2.48 us -> 0.69 us
    pallas_call x4 -> x5, Pallas kernels: 19.5 us -> 13.6 us  [call(): pl.pallas_call(functools.partial(kernel, **params), in_specs=[pl.BlockSpe...]
    all_to_all x1, waiting for transfers between devices: 7.78 us -> 2.55 us  [body(): lax.all_to_all(send.reshape(slabs, 1, 9 * LANES), 'slab', 0, 0, tiled=True)]
    all_to_all x1, starting transfers between devices: 11.7 us -> 15.2 us  [body(): lax.all_to_all(send.reshape(slabs, 1, 9 * LANES), 'slab', 0, 0, tiled=True)]
    ppermute x2 -> x5, starting transfers between devices: 6.42 us -> 9.52 us  [the longest x3 4.93 us: body(): lax.ppermute(trace, 'probe', [(i, (i + k) % groups) for i in range(groups)])]
    slice x2 -> x0, local copies, waits for them, and re-layouts: 2.17 us -> none  [the longest x1 1.19 us: body(): return (adjoint, observed, total[0, 0] / count)]
    ppermute x2 -> x5, waiting for transfers between devices: 4.34 us -> 6.39 us  [the longest x3 3.26 us: body(): lax.ppermute(trace, 'probe', [(i, (i + k) % groups) for i in range(groups)])]
    unnamed x6 -> x0, local copies, waits for them, and re-layouts: 1.46 us -> none
  transfers between devices with their start and end apart: 3 -> 6, of which waited for: 2 -> 4; matrix products, arithmetic and copies ran while one was open for 0% -> 0% of each run, Pallas kernels for 12% -> 11%
where the time goes in v2:
time: 48.2 us; the launch traced here: 47.9 us
  starting transfers between devices  24.7 us (51%)
  Pallas kernels  13.6 us (28%)
  waiting for transfers between devices  8.95 us (19%)
  between operations  0.69 us (1%)
    all_to_all x1, starting transfers between devices, body(): lax.all_to_all(send.reshape(slabs, 1, 9 * LANES), 'slab', 0, 0, tiled=True)  15.2 us
    pallas_call x5, Pallas kernels, call(): pl.pallas_call(functools.partial(kernel, **params), in_specs=[pl.BlockSpe...  13.6 us
    ppermute x3, starting transfers between devices, body(): lax.ppermute(trace, 'probe', [(i, (i + k) % groups) for i in range(groups)])  4.93 us
    ppermute x3, waiting for transfers between devices, body(): lax.ppermute(trace, 'probe', [(i, (i + k) % groups) for i in range(groups)])  3.26 us
    ppermute x1, waiting for transfers between devices, body(): cross = lax.ppermute(to_cross, 'slab', swap_cross)  3.13 us
    ppermute x1, starting transfers between devices, body(): cross = lax.ppermute(to_cross, 'slab', swap_cross)  3.13 us
    all_to_all x1, waiting for transfers between devices, body(): lax.all_to_all(send.reshape(slabs, 1, 9 * LANES), 'slab', 0, 0, tiled=True)  2.55 us
    ppermute x1, starting transfers between devices, body(): same = lax.ppermute(to_same, 'slab', swap_same)  1.46 us
  transfers between devices with their start and end apart: 6, of which 4 were waited for; matrix products, arithmetic and copies ran while one was open for 0% of the time, Pallas kernels for 11%

profile of v2, /device:TPU:1, one launch (start us, length us, event | category | flops | bytes accessed | tf_op | source)
XLA Modules:
  0.0 47.9 jit_solution(9448806232095053268)
XLA Ops:
  0.6 6.5 %shard_map.94 = (f32[64,512]{1,0:T(8,128)S(1)}, f32[64,512]{1,0:T(8,128)S(1)}, f32[64,512]{1,0:T(8,128)S(1)}, f32[64,512]{1,0:T(8,128)S(1)}, f32[16,1024]{1,0:T(...) custom-call(s32[1]{0:T(128)} %bitcast.slab_ref.at_ref, s32[32,128]{1,0:T(8,128)} %bitcast.19, s32[32,128]{1,0:T(8,128)} %bitcast.20, ...), custom_call_target="tpu_custom_call" | custom-call | tf_op jit(solution)/shard_map/pallas_call | solution.py:310
  7.2 1.5 %collective-permute-start = (f32[64,512]{1,0:T(8,128)S(1)}, f32[64,512]{1,0:T(8,128)S(1)}, u32[]{:S(2)}, u32[]{:S(2)}) collective-permute-start(f32[64,512]{1,0:T(8,128)S(1)} %get-tuple-element.17), channel_id=1, source_target_pairs={{0,4},{4,0},{8,12},{12,8},{16,20},{20,16},{24,28},{28,24},{32,36},... | collective-permute-start | bytes 393224 | tf_op jit(solution)/shard_map/ppermute | solution.py:344
  8.6 3.1 %collective-permute-start.1 = (f32[64,512]{1,0:T(8,128)S(1)}, f32[64,512]{1,0:T(8,128)S(1)}, u32[]{:S(2)}, u32[]{:S(2)}) collective-permute-start(f32[64,512]{1,0:T(8,128)S(1)} %get-tuple-element.18), channel_id=1, source_target_pairs={{4,8},{8,4},{12,16},{16,12},{20,24},{24,20},{28,32},{32,28},{36,40... | collective-permute-start | bytes 393224 | tf_op jit(solution)/shard_map/ppermute | solution.py:343
  11.7 0.0 collective-permute-done.same_ref
  11.8 3.1 %collective-permute-done.1.cross_ref = f32[64,512]{1,0:T(8,128)S(1)} collective-permute-done((f32[64,512]{1,0:T(8,128)S(1)}, f32[64,512]{1,0:T(8,128)S(1)}, u32[]{:S(2)}, u32[]{:S(2)}) %collective-permute-start.1) | collective-permute-done | bytes 131104 | tf_op jit(solution)/shard_map/ppermute | solution.py:343
  14.9 0.3 shard_map.95
  15.2 4.2 %collective-permute-start.4 = (f32[8,128]{1,0:T(8,128)S(1)}, f32[8,128]{1,0:T(8,128)S(1)}, u32[]{:S(2)}, u32[]{:S(2)}) collective-permute-start(f32[8,128]{1,0:T(8,128)S(1)} %get-tuple-element.23.refs_0_), channel_id=1, source_target_pairs={{0,3},{1,0},{2,1},{3,2},{4,7},{5,4},{6,5},{7,6},{8,11},{9,8},{10,9... | collective-permute-start | bytes 12296 | tf_op jit(solution)/shard_map/ppermute | solution.py:352
  19.4 0.0 collective-permute-start.3
  19.4 0.7 %collective-permute-start.2 = (f32[8,128]{1,0:T(8,128)S(1)}, f32[8,128]{1,0:T(8,128)S(1)}, u32[]{:S(2)}, u32[]{:S(2)}) collective-permute-start(f32[8,128]{1,0:T(8,128)S(1)} %get-tuple-element.23.refs_0_), channel_id=1, source_target_pairs={{0,1},{1,2},{2,3},{3,0},{4,5},{5,6},{6,7},{7,4},{8,9},{9,10},{10,1... | collective-permute-start | bytes 12296 | tf_op jit(solution)/shard_map/ppermute | solution.py:352
  20.1 0.1 collective-permute-done.4.refs_3_
  20.2 3.2 %collective-permute-done.3.refs_2_ = f32[8,128]{1,0:T(8,128)S(1)} collective-permute-done((f32[8,128]{1,0:T(8,128)S(1)}, f32[8,128]{1,0:T(8,128)S(1)}, u32[]{:S(2)}, u32[]{:S(2)}) %collective-permute-start.3) | collective-permute-done | bytes 4128 | tf_op jit(solution)/shard_map/ppermute | solution.py:352
  23.4 0.0 collective-permute-done.2.refs_1_
  23.4 0.7 %shard_map.97 = f32[288,128]{1,0:T(8,128)} custom-call(f32[256,128]{1,0:T(8,128)S(1)} %get-tuple-element.22.block_ref, f32[8,128]{1,0:T(8,128)S(1)} %get-tuple-element.23.refs_0_, f32[8,128]{1,0:T(8,128)S(1)} %collective-permute-done.2.refs_1_, f32[8,128]{1,0:T(8,128)S(1)} %collective-permute-done.3.refs_2_, f32[8,128]{1,0:T(8,128)S(1)} %collective-permute-done.4.refs_3_), custom_call_target="tpu_custom_call" | custom-call | tf_op jit(solution)/shard_map/pallas_call | solution.py:310
  24.1 15.2 %all-to-all-start = ((f32[32,1,1152]{2,1,0:T(1,128)}), f32[32,1,1152]{2,1,0:T(1,128)S(1)}, u32[]{:S(2)}, u32[]{:S(2)}) async-start(f32[32,1,1152]{2,1,0:T(1,128)} %bitcast.11), calls=%async_computation | async-start | bytes 294912 | tf_op jit(solution)/shard_map/all_to_all | solution.py:354
  39.2 5.2 %shard_map.96 = bf16[16,4,64,4,128]{4,3,2,1,0:T(4,128)(2,1)} custom-call(bf16[256,1024]{1,0:T(8,128)(2,1)S(1)} %get-tuple-element.20.src_ref, f32[16,1024]{1,0:T(8,128)S(1)} %get-tuple-element.19.meta_ref, s32[1]{0:T(128)} %get-tuple-element.21.flag_ref), custom_call_target="tpu_custom_call" | custom-call | tf_op jit(solution)/shard_map/pallas_call | solution.py:310
  44.4 2.6 %all-to-all-done = f32[32,1,1152]{2,1,0:T(1,128)S(1)} async-done(((f32[32,1,1152]{2,1,0:T(1,128)}), f32[32,1,1152]{2,1,0:T(1,128)S(1)}, u32[]{:S(2)}, u32[]{:S(2)}) %all-to-all-start) | async-done | bytes 147488 | tf_op jit(solution)/shard_map/all_to_all | solution.py:354
  47.0 0.9 %shard_map.98 = (f32[64,128]{1,0:T(8,128)}, f32[1,1]{1,0:T(1,128)}) custom-call(f32[288,128]{1,0:T(8,128)S(1)} %bitcast.16, f32[8,128]{1,0:T(8,128)S(1)} %get-tuple-element.24.place_ref), custom_call_target="tpu_custom_call" | custom-call | tf_op jit(solution)/shard_map/pallas_call | solution.py:310
Async XLA Ops:
  7.2 4.6 %collective-permute-start = (f32[64,512]{1,0:T(8,128)S(1)}, f32[64,512]{1,0:T(8,128)S(1)}, u32[]{:S(2)}, u32[]{:S(2)}) collective-permute-start(f32[64,512]{1,0:T(8,128)S(1)} %get-tuple-element.17), channel_id=1, source_target_pairs={{0,4},{4,0},{8,12},{12,8},{16,20},{20,16},{24,28},{28,24},{32,36},... | collective-permute-start | bytes 393224 | tf_op jit(solution)/shard_map/ppermute | solution.py:344
  8.6 6.3 %collective-permute-start.1 = (f32[64,512]{1,0:T(8,128)S(1)}, f32[64,512]{1,0:T(8,128)S(1)}, u32[]{:S(2)}, u32[]{:S(2)}) collective-permute-start(f32[64,512]{1,0:T(8,128)S(1)} %get-tuple-element.18), channel_id=1, source_target_pairs={{4,8},{8,4},{12,16},{16,12},{20,24},{24,20},{28,32},{32,28},{36,40... | collective-permute-start | bytes 393224 | tf_op jit(solution)/shard_map/ppermute | solution.py:343
  15.2 5.0 %collective-permute-start.4 = (f32[8,128]{1,0:T(8,128)S(1)}, f32[8,128]{1,0:T(8,128)S(1)}, u32[]{:S(2)}, u32[]{:S(2)}) collective-permute-start(f32[8,128]{1,0:T(8,128)S(1)} %get-tuple-element.23.refs_0_), channel_id=1, source_target_pairs={{0,3},{1,0},{2,1},{3,2},{4,7},{5,4},{6,5},{7,6},{8,11},{9,8},{10,9... | collective-permute-start | bytes 12296 | tf_op jit(solution)/shard_map/ppermute | solution.py:352
  19.4 4.0 %collective-permute-start.3 = (f32[8,128]{1,0:T(8,128)S(1)}, f32[8,128]{1,0:T(8,128)S(1)}, u32[]{:S(2)}, u32[]{:S(2)}) collective-permute-start(f32[8,128]{1,0:T(8,128)S(1)} %get-tuple-element.23.refs_0_), channel_id=1, source_target_pairs={{0,2},{1,3},{2,0},{3,1},{4,6},{5,7},{6,4},{7,5},{8,10},{9,11},{10,... | collective-permute-start | bytes 12296 | tf_op jit(solution)/shard_map/ppermute | solution.py:352
  19.4 4.0 %collective-permute-start.2 = (f32[8,128]{1,0:T(8,128)S(1)}, f32[8,128]{1,0:T(8,128)S(1)}, u32[]{:S(2)}, u32[]{:S(2)}) collective-permute-start(f32[8,128]{1,0:T(8,128)S(1)} %get-tuple-element.23.refs_0_), channel_id=1, source_target_pairs={{0,1},{1,2},{2,3},{3,0},{4,5},{5,6},{6,7},{7,4},{8,9},{9,10},{10,1... | collective-permute-start | bytes 12296 | tf_op jit(solution)/shard_map/ppermute | solution.py:352
  24.1 22.9 %all-to-all-start = ((f32[32,1,1152]{2,1,0:T(1,128)}), f32[32,1,1152]{2,1,0:T(1,128)S(1)}, u32[]{:S(2)}, u32[]{:S(2)}) async-start(f32[32,1,1152]{2,1,0:T(1,128)} %bitcast.11), calls=%async_computation | async-start | bytes 294912 | tf_op jit(solution)/shard_map/all_to_all | solution.py:354

commit v3 on v2

--- a/solution.py
+++ b/solution.py
@@ -11,8 +11,8 @@
 BF16 = jnp.bfloat16
 LANES = 128
 SLOTS = 16
-VMEM_LIMIT = 60 * 2**20
-CHUNKS = 1
+VMEM_LIMIT = 32 * 2**20
+CHUNKS = 2
 OUT_CHUNKS = 8
 
 
@@ -31,13 +31,6 @@
 def pieces(x):
     high = x.astype(BF16)
     return high, (x - high.astype(F32)).astype(BF16)
-
-
-def pieces3(x):
-    high = x.astype(BF16)
-    rest = x - high.astype(F32)
-    mid = rest.astype(BF16)
-    return high, mid, (rest - mid.astype(F32)).astype(BF16)
 
 
 def lookup_rows(order_hi, order_lo, rows):
@@ -139,8 +132,8 @@
 
 def forward_kernel(
     slab_ref, rows_hbm, cols_hbm, rf_hbm, cf_hbm, w_hbm, order_hbm, u_ref,
-    own_ref, last_ref, same_ref, cross_ref, meta_ref, place_ref, flag_ref,
-    scr, small_i, small_f, sem, small_sem,
+    last_ref, same_ref, cross_ref, own_ref, meta_ref, place_ref, flag_ref, scr,
+    small_i, small_f, sem, small_sem,
 ):
     chunks = CHUNKS
     width = scr.shape[1] // chunks
@@ -169,12 +162,12 @@
     order_lo = order % LANES
     rows = small_i[1]
     owned_rows = lookup_rows(order_hi, order_lo, rows)
-    count = own_ref.shape[1]
+    count = last_ref.shape[1]
     skip = count // 2
     given = (order_hi, order_lo, rows, small_i[2], small_f[0], small_f[1], small_f[2])
-    own_slots, _ = owner_slots(slab, owned_rows)
-    last_slots, many = owner_slots(slab - 1, owned_rows)
-    flag_ref[0] = (many > 0.5).astype(jnp.int32)
+    own_slots, own_many = owner_slots(slab, owned_rows)
+    last_slots, last_many = owner_slots(slab - 1, owned_rows)
+    flag_ref[0] = (jnp.maximum(own_many, last_many) > 0.5).astype(jnp.int32)
     meta = slot_fields(slab, (own_slots, last_slots), ((0, 0), (0, 1), (1, 1)), *given)
     meta_ref[:, :count] = meta[:, :count]
     meta_ref[:, count : count + skip] = jnp.zeros((16, skip), F32)
@@ -188,28 +181,27 @@
     rank = jnp.where(on_last > 0.5, SLOTS - 1.0 - rank, rank)
     half = jnp.where(rank >= 8.0, 1.0, 0.0)
     place_ref[...] = jnp.concatenate([own * 8.0 + rank - 8.0 * half, half] + [jnp.zeros_like(own)] * 6, axis=0)
-    main, carry, tile16 = column_parts(meta)
-    sums = [jnp.zeros((256, count), F32)] + [jnp.zeros((128, skip), F32)] * 2
+    near = meta[:, skip:]
+    main, carry, tile16 = column_parts(near)
+    acc = jnp.zeros((256, count), F32)
     for c in range(chunks):
         for k in range(4):
             copy(c, k).wait()
         for n in range(c * width // 2, (c + 1) * width // 2):
-            block = field_block(scr, n)
-            table = column_table(n, tile16, main, carry)
-            sums[0] = sums[0] + dot(block, table[:, :count])
-            for m in (0, 1):
-                sums[1 + m] = sums[1 + m] + dot(block[128 * m : 128 * m + 128], table[:, count:])
-    acc = jnp.concatenate([sums[0], jnp.concatenate(sums[1:], axis=0)], axis=1)
-    part = row_sum(acc * row_sides(meta), 4)
+            acc = acc + dot(field_block(scr, n), column_table(n, tile16, main, carry))
+    part = row_sum(acc * row_sides(near), 4)
     even = slab % 2 == 0
-
-    def give(own_part, last_part):
-        last_ref[...] = last_part
-        same_ref[...] = jnp.where(even, own_part, last_part)
-        cross_ref[...] = jnp.where(even, last_part, own_part)
-
-    own_ref[...] = part[:, :count]
-    give(part[:, :count], jnp.concatenate([jnp.zeros((64, skip), F32), part[:, count:]], axis=1))
+    own_ref[...] = part[:, :skip]
+
+    def give(own_first, last_first, part):
+        own = jnp.concatenate([own_first, part[:, :skip]], axis=1)
+        last = jnp.concatenate([last_first, part[:, skip:]], axis=1)
+        last_ref[...] = last
+        same_ref[...] = jnp.where(even, own, last)
+        cross_ref[...] = jnp.where(even, last, own)
+
+    nothing = jnp.zeros((64, skip), F32)
+    give(nothing, nothing, part)
 
     @pl.when(flag_ref[0] != 0)
     def _():
@@ -219,24 +211,38 @@
         rows = small_i[1]
         slots, _ = owner_slots(slab - 1, lookup_rows(order_hi, order_lo, rows))
         given = (order_hi, order_lo, rows, small_i[2], small_f[0], small_f[1], small_f[2])
-        far_meta = slot_fields(slab, (slots,), ((0, 0),), *given)
-        meta_ref[:, count : count + skip] = far_meta
-        far_main, far_carry, _ = column_parts(far_meta)
-        far_tile = jnp.broadcast_to(far_meta[:1], (16, skip))
-
-        def step(n, far):
-            return far + dot(field_block(scr, n), column_table(n, far_tile, far_main, far_carry))
-
-        far = lax.fori_loop(0, scr.shape[1] // 2, step, jnp.zeros((256, skip), F32))
-        give(own_ref[...], jnp.concatenate([row_sum(far * row_sides(far_meta), 4), last_ref[:, skip:]], axis=1))
-
-
-def combine_kernel(own_ref, last_ref, same_ref, cross_ref, meta_ref, at_ref, block_ref, trace_ref, src_ref):
-    count = own_ref.shape[1]
+        meta_ref[:, count : count + skip] = slot_fields(slab, (slots,), ((0, 0),), *given)
+        far = jnp.concatenate([meta_ref[:, :skip], meta_ref[:, count : count + skip]], axis=1)
+        far_main, far_carry, _ = column_parts(far)
+        far_tile = jnp.broadcast_to(far[:1], (16, count))
+
+        def step(n, acc):
+            return acc + dot(field_block(scr, n), column_table(n, far_tile, far_main, far_carry))
+
+        acc = lax.fori_loop(0, scr.shape[1] // 2, step, jnp.zeros((256, count), F32))
+        first = row_sum(acc * row_sides(far), 4)
+        give(first[:, :skip], first[:, skip:], jnp.concatenate([own_ref[...], last_ref[:, skip:]], axis=1))
+
+
+def rest_kernel(scr, meta_ref, part_ref):
+    meta = meta_ref[:, : part_ref.shape[1]]
+    main, carry, tile16 = column_parts(meta)
+    sums = [jnp.zeros((128, part_ref.shape[1]), F32)] * 2
+    for n in range(scr.shape[1] // 2):
+        block = field_block(scr, n)
+        table = column_table(n, tile16, main, carry)
+        for m in (0, 1):
+            sums[m] = sums[m] + dot(block[128 * m : 128 * m + 128], table)
+    part_ref[...] = row_sum(jnp.concatenate(sums, axis=0) * row_sides(meta), 4)
+
+
+def combine_kernel(rest_ref, own_ref, last_ref, same_ref, cross_ref, meta_ref, at_ref, block_ref, trace_ref, src_ref):
+    count = last_ref.shape[1]
     even = at_ref[0] % 2 == 0
+    own = jnp.concatenate([rest_ref[...], own_ref[...]], axis=1)
     same = same_ref[...]
     cross = cross_ref[...]
-    value = own_ref[...] + jnp.where(even, same, cross)
+    value = own + jnp.where(even, same, cross)
     before = last_ref[...] + jnp.where(even, cross, same)
     weight = meta_ref[8:9, :]
     spread = jnp.concatenate([value, before], axis=1) * weight
@@ -298,15 +304,16 @@
     slabs = got_ref.shape[0] // 9
     values = jnp.concatenate([got_ref[9 * q : 9 * q + 8, :] for q in range(slabs)], axis=0)
     pick = one_hot(iota((8 * slabs, LANES), 0).astype(F32) == place_ref[0:1, :])
-    found = sum(dot(part, pick, ((0,), (0,))) for part in pieces3(values))
+    found = sum(dot(part, pick, ((0,), (0,))) for part in pieces(values))
     observed_ref[...] = jnp.where(place_ref[1:2, :] > 0.5, found[64:], found[:64])
     traces = jnp.sum(got_ref[pl.ds(8, slabs, stride=9), :], axis=0, keepdims=True)
     total_ref[...] = traces[:, :1] * scale
 
 
 def call(kernel, inputs, outs, scratch=(), **params):
-    kinds = {"v": pltpu.VMEM, "s": pltpu.SMEM, "h": pl.ANY, "w": pltpu.VMEM}
-    arrays = [pltpu.with_memory_space_constraint(x, pltpu.VMEM) if k == "w" else x for k, x in inputs]
+    kinds = {"v": pltpu.VMEM, "s": pltpu.SMEM, "h": pltpu.HBM, "w": pltpu.VMEM}
+    held = {"w": pltpu.VMEM, "h": pltpu.HBM}
+    arrays = [pltpu.with_memory_space_constraint(x, held[k]) if k in held else x for k, x in inputs]
     return pl.pallas_call(
         functools.partial(kernel, **params),
         in_specs=[pl.BlockSpec(memory_space=kinds[k]) for k, _ in inputs],
@@ -325,13 +332,14 @@
     tiles = probe_fields.shape[2] // LANES
     fields = probe_fields.reshape(16, 4, 4, tiles, LANES).transpose(0, 1, 3, 2, 4)
     flat = [x.reshape(slabs, LANES) for x in (sensor_rows, sensor_cols, row_frac, col_frac, sensor_weights, owner_order)]
-    own, last, to_same, to_cross, meta, place, flag = call(
+    half = per_list // 2
+    last, to_same, to_cross, own, meta, place, flag, lines = call(
         forward_kernel,
         [("s", at)] + [("h", x) for x in flat] + [("h", fields)],
-        [("w", (64, per_list), F32)] * 4
-        + [("w", (16, 2 * per_list), F32), ("w", (8, LANES), F32), ("s", (1,), jnp.int32)],
+        [("w", (64, per_list), F32)] * 3
+        + [("w", (64, half), F32), ("w", (16, 2 * per_list), F32), ("w", (8, LANES), F32), ("s", (1,), jnp.int32)]
+        + [("w", (16, tiles, 16, LANES), BF16)],
         [
-            pltpu.VMEM((16, tiles, 16, LANES), BF16),
             pltpu.VMEM((3, slabs, LANES), jnp.int32),
             pltpu.VMEM((3, slabs, LANES), F32),
             pltpu.SemaphoreType.DMA((CHUNKS, 4)),
@@ -342,9 +350,10 @@
     swap_same = [(i, i - 1 if i % 2 else i + 1) for i in range(slabs)]
     cross = lax.ppermute(to_cross, "slab", swap_cross)
     same = lax.ppermute(to_same, "slab", swap_same)
+    (rest,) = call(rest_kernel, [("w", lines), ("w", meta)], [("w", (64, half), F32)])
     blocks, trace, sources = call(
         combine_kernel,
-        [("w", own), ("w", last), ("w", same), ("w", cross), ("w", meta), ("s", at)],
+        [("w", rest), ("w", own), ("w", last), ("w", same), ("w", cross), ("w", meta), ("s", at)],
         [("w", (8 * slabs, LANES), F32), ("w", (8, LANES), F32), ("w", (256, 2 * per_list), BF16)],
     )
     traces = [trace]

time: 48.2 us -> 49.4 us (1.025)
  starting transfers between devices: 24.7 us -> 27.1 us
  waiting for transfers between devices: 8.95 us -> 7.55 us
    all_to_all x1, starting transfers between devices: 15.2 us -> 17.6 us  [body(): lax.all_to_all(send.reshape(slabs, 1, 9 * LANES), 'slab', 0, 0, tiled=True)]
    ppermute x1, waiting for transfers between devices: 3.13 us -> 1.69 us  [body(): cross = lax.ppermute(to_cross, 'slab', swap_cross)]
    pallas_call x5 -> x6, Pallas kernels: 13.6 us -> 13.8 us  [call(): pl.pallas_call(functools.partial(kernel, **params), in_specs=[pl.BlockSpe...]
  transfers between devices with their start and end apart: 6 -> 6, of which waited for: 4 -> 4; matrix products, arithmetic and copies ran while one was open for 0% -> 0% of each run, Pallas kernels for 11% -> 13%
where the time goes in v3:
time: 49.4 us; the launch traced here: 49.1 us
  starting transfers between devices  27.1 us (55%)
  Pallas kernels  13.8 us (28%)
  waiting for transfers between devices  7.55 us (15%)
  between operations  0.69 us (1%)
    all_to_all x1, starting transfers between devices, body(): lax.all_to_all(send.reshape(slabs, 1, 9 * LANES), 'slab', 0, 0, tiled=True)  17.6 us
    pallas_call x6, Pallas kernels, call(): pl.pallas_call(functools.partial(kernel, **params), in_specs=[pl.BlockSpe...  13.8 us
    ppermute x3, starting transfers between devices, body(): lax.ppermute(trace, 'probe', [(i, (i + k) % groups) for i in range(groups)])  4.9 us
    ppermute x3, waiting for transfers between devices, body(): lax.ppermute(trace, 'probe', [(i, (i + k) % groups) for i in range(groups)])  3.29 us
    ppermute x1, starting transfers between devices, body(): cross = lax.ppermute(to_cross, 'slab', swap_cross)  3.13 us
    all_to_all x1, waiting for transfers between devices, body(): lax.all_to_all(send.reshape(slabs, 1, 9 * LANES), 'slab', 0, 0, tiled=True)  2.56 us
    ppermute x1, waiting for transfers between devices, body(): cross = lax.ppermute(to_cross, 'slab', swap_cross)  1.69 us
    ppermute x1, starting transfers between devices, body(): same = lax.ppermute(to_same, 'slab', swap_same)  1.46 us
  transfers between devices with their start and end apart: 6, of which 4 were waited for; matrix products, arithmetic and copies ran while one was open for 0% of the time, Pallas kernels for 13%

profile of v3, /device:TPU:1, one launch (start us, length us, event | category | flops | bytes accessed | tf_op | source)
XLA Modules:
  0.0 49.1 jit_solution(1890326801219637896)
XLA Ops:
  0.6 5.3 %shard_map.94 = (f32[64,512]{1,0:T(8,128)S(1)}, f32[64,512]{1,0:T(8,128)S(1)}, f32[64,512]{1,0:T(8,128)S(1)}, f32[64,256]{1,0:T(8,128)S(1)}, f32[16,1024]{1,0:T(...) custom-call(s32[1]{0:T(128)} %bitcast.slab_ref.at_ref, s32[32,128]{1,0:T(8,128)} %bitcast.19, ...), custom_call_target="tpu_custom_call" | custom-call | tf_op jit(solution)/shard_map/pallas_call | solution.py:317
  6.0 1.5 %collective-permute-start = (f32[64,512]{1,0:T(8,128)S(1)}, f32[64,512]{1,0:T(8,128)S(1)}, u32[]{:S(2)}, u32[]{:S(2)}) collective-permute-start(f32[64,512]{1,0:T(8,128)S(1)} %get-tuple-element.20), channel_id=1, source_target_pairs={{0,4},{4,0},{8,12},{12,8},{16,20},{20,16},{24,28},{28,24},{32,36},... | collective-permute-start | bytes 393224 | tf_op jit(solution)/shard_map/ppermute | solution.py:352
  7.4 3.1 %collective-permute-start.1 = (f32[64,512]{1,0:T(8,128)S(1)}, f32[64,512]{1,0:T(8,128)S(1)}, u32[]{:S(2)}, u32[]{:S(2)}) collective-permute-start(f32[64,512]{1,0:T(8,128)S(1)} %get-tuple-element.21), channel_id=1, source_target_pairs={{4,8},{8,4},{12,16},{16,12},{20,24},{24,20},{28,32},{32,28},{36,40... | collective-permute-start | bytes 393224 | tf_op jit(solution)/shard_map/ppermute | solution.py:351
  10.6 1.4 %shard_map.95.rest_ref = f32[64,256]{1,0:T(8,128)S(1)} custom-call(bf16[16,64,16,128]{3,2,1,0:T(8,128)(2,1)S(1)} %get-tuple-element.16.scr, f32[16,1024]{1,0:T(8,128)S(1)} %get-tuple-element.17.meta_ref), custom_call_target="tpu_custom_call" | custom-call | tf_op jit(solution)/shard_map/pallas_call | solution.py:317
  12.0 0.0 collective-permute-done.same_ref
  12.0 1.7 %collective-permute-done.1.cross_ref = f32[64,512]{1,0:T(8,128)S(1)} collective-permute-done((f32[64,512]{1,0:T(8,128)S(1)}, f32[64,512]{1,0:T(8,128)S(1)}, u32[]{:S(2)}, u32[]{:S(2)}) %collective-permute-start.1) | collective-permute-done | bytes 131104 | tf_op jit(solution)/shard_map/ppermute | solution.py:351
  13.7 0.3 shard_map.96
  14.0 4.2 %collective-permute-start.4 = (f32[8,128]{1,0:T(8,128)S(1)}, f32[8,128]{1,0:T(8,128)S(1)}, u32[]{:S(2)}, u32[]{:S(2)}) collective-permute-start(f32[8,128]{1,0:T(8,128)S(1)} %get-tuple-element.25.refs_0_), channel_id=1, source_target_pairs={{0,3},{1,0},{2,1},{3,2},{4,7},{5,4},{6,5},{7,6},{8,11},{9,8},{10,9... | collective-permute-start | bytes 12296 | tf_op jit(solution)/shard_map/ppermute | solution.py:361
  18.3 0.0 collective-permute-start.3
  18.3 0.7 %collective-permute-start.2 = (f32[8,128]{1,0:T(8,128)S(1)}, f32[8,128]{1,0:T(8,128)S(1)}, u32[]{:S(2)}, u32[]{:S(2)}) collective-permute-start(f32[8,128]{1,0:T(8,128)S(1)} %get-tuple-element.25.refs_0_), channel_id=1, source_target_pairs={{0,1},{1,2},{2,3},{3,0},{4,5},{5,6},{6,7},{7,4},{8,9},{9,10},{10,1... | collective-permute-start | bytes 12296 | tf_op jit(solution)/shard_map/ppermute | solution.py:361
  18.9 0.1 collective-permute-done.4.refs_3_
  19.0 3.2 %collective-permute-done.3.refs_2_ = f32[8,128]{1,0:T(8,128)S(1)} collective-permute-done((f32[8,128]{1,0:T(8,128)S(1)}, f32[8,128]{1,0:T(8,128)S(1)}, u32[]{:S(2)}, u32[]{:S(2)}) %collective-permute-start.3) | collective-permute-done | bytes 4128 | tf_op jit(solution)/shard_map/ppermute | solution.py:361
  22.2 0.0 collective-permute-done.2.refs_1_
  22.2 0.7 %shard_map.98 = f32[288,128]{1,0:T(8,128)} custom-call(f32[256,128]{1,0:T(8,128)S(1)} %get-tuple-element.24.block_ref, f32[8,128]{1,0:T(8,128)S(1)} %get-tuple-element.25.refs_0_, f32[8,128]{1,0:T(8,128)S(1)} %collective-permute-done.2.refs_1_, f32[8,128]{1,0:T(8,128)S(1)} %collective-permute-done.3.refs_2_, f32[8,128]{1,0:T(8,128)S(1)} %collective-permute-done.4.refs_3_), custom_call_target="tpu_custom_call" | custom-call | tf_op jit(solution)/shard_map/pallas_call | solution.py:317
  22.9 17.6 %all-to-all-start = ((f32[32,1,1152]{2,1,0:T(1,128)}), f32[32,1,1152]{2,1,0:T(1,128)S(1)}, u32[]{:S(2)}, u32[]{:S(2)}) async-start(f32[32,1,1152]{2,1,0:T(1,128)} %bitcast.11), calls=%async_computation | async-start | bytes 294912 | tf_op jit(solution)/shard_map/all_to_all | solution.py:363
  40.5 5.2 %shard_map.97 = bf16[16,4,64,4,128]{4,3,2,1,0:T(4,128)(2,1)} custom-call(bf16[256,1024]{1,0:T(8,128)(2,1)S(1)} %get-tuple-element.22.src_ref, f32[16,1024]{1,0:T(8,128)S(1)} %get-tuple-element.17.meta_ref, s32[1]{0:T(128)} %get-tuple-element.23.flag_ref), custom_call_target="tpu_custom_call" | custom-call | tf_op jit(solution)/shard_map/pallas_call | solution.py:317
  45.7 2.6 %all-to-all-done = f32[32,1,1152]{2,1,0:T(1,128)S(1)} async-done(((f32[32,1,1152]{2,1,0:T(1,128)}), f32[32,1,1152]{2,1,0:T(1,128)S(1)}, u32[]{:S(2)}, u32[]{:S(2)}) %all-to-all-start) | async-done | bytes 147488 | tf_op jit(solution)/shard_map/all_to_all | solution.py:363
  48.2 0.8 %shard_map.99 = (f32[64,128]{1,0:T(8,128)}, f32[1,1]{1,0:T(1,128)}) custom-call(f32[288,128]{1,0:T(8,128)S(1)} %bitcast.16, f32[8,128]{1,0:T(8,128)S(1)} %get-tuple-element.26.place_ref), custom_call_target="tpu_custom_call" | custom-call | tf_op jit(solution)/shard_map/pallas_call | solution.py:317
Async XLA Ops:
  6.0 6.0 %collective-permute-start = (f32[64,512]{1,0:T(8,128)S(1)}, f32[64,512]{1,0:T(8,128)S(1)}, u32[]{:S(2)}, u32[]{:S(2)}) collective-permute-start(f32[64,512]{1,0:T(8,128)S(1)} %get-tuple-element.20), channel_id=1, source_target_pairs={{0,4},{4,0},{8,12},{12,8},{16,20},{20,16},{24,28},{28,24},{32,36},... | collective-permute-start | bytes 393224 | tf_op jit(solution)/shard_map/ppermute | solution.py:352
  7.4 6.3 %collective-permute-start.1 = (f32[64,512]{1,0:T(8,128)S(1)}, f32[64,512]{1,0:T(8,128)S(1)}, u32[]{:S(2)}, u32[]{:S(2)}) collective-permute-start(f32[64,512]{1,0:T(8,128)S(1)} %get-tuple-element.21), channel_id=1, source_target_pairs={{4,8},{8,4},{12,16},{16,12},{20,24},{24,20},{28,32},{32,28},{36,40... | collective-permute-start | bytes 393224 | tf_op jit(solution)/shard_map/ppermute | solution.py:351
  14.0 5.0 %collective-permute-start.4 = (f32[8,128]{1,0:T(8,128)S(1)}, f32[8,128]{1,0:T(8,128)S(1)}, u32[]{:S(2)}, u32[]{:S(2)}) collective-permute-start(f32[8,128]{1,0:T(8,128)S(1)} %get-tuple-element.25.refs_0_), channel_id=1, source_target_pairs={{0,3},{1,0},{2,1},{3,2},{4,7},{5,4},{6,5},{7,6},{8,11},{9,8},{10,9... | collective-permute-start | bytes 12296 | tf_op jit(solution)/shard_map/ppermute | solution.py:361
  18.3 4.0 %collective-permute-start.3 = (f32[8,128]{1,0:T(8,128)S(1)}, f32[8,128]{1,0:T(8,128)S(1)}, u32[]{:S(2)}, u32[]{:S(2)}) collective-permute-start(f32[8,128]{1,0:T(8,128)S(1)} %get-tuple-element.25.refs_0_), channel_id=1, source_target_pairs={{0,2},{1,3},{2,0},{3,1},{4,6},{5,7},{6,4},{7,5},{8,10},{9,11},{10,... | collective-permute-start | bytes 12296 | tf_op jit(solution)/shard_map/ppermute | solution.py:361
  18.3 4.0 %collective-permute-start.2 = (f32[8,128]{1,0:T(8,128)S(1)}, f32[8,128]{1,0:T(8,128)S(1)}, u32[]{:S(2)}, u32[]{:S(2)}) collective-permute-start(f32[8,128]{1,0:T(8,128)S(1)} %get-tuple-element.25.refs_0_), channel_id=1, source_target_pairs={{0,1},{1,2},{2,3},{3,0},{4,5},{5,6},{6,7},{7,4},{8,9},{9,10},{10,1... | collective-permute-start | bytes 12296 | tf_op jit(solution)/shard_map/ppermute | solution.py:361
  22.9 25.3 %all-to-all-start = ((f32[32,1,1152]{2,1,0:T(1,128)}), f32[32,1,1152]{2,1,0:T(1,128)S(1)}, u32[]{:S(2)}, u32[]{:S(2)}) async-start(f32[32,1,1152]{2,1,0:T(1,128)} %bitcast.11), calls=%async_computation | async-start | bytes 294912 | tf_op jit(solution)/shard_map/all_to_all | solution.py:363

commit v4 on v3

--- a/solution.py
+++ b/solution.py
@@ -48,18 +48,18 @@
     last = match & (owned_rows % 4 == 3)
     rank = dot(one_hot(match & ~last), upper)
     back_rank = dot(one_hot(last), upper)
-    many = jnp.max(jnp.where(last & (back_rank > 7.5), 1.0, 0.0))
+    many = jnp.max(jnp.where(last, back_rank + 1.0, 0.0))
     return jnp.where(last, SLOTS - 1.0 - back_rank, jnp.where(match, rank, -1.0)).astype(BF16), many
 
 
 def slot_fields(slab, slots, pieces_of, order_hi, order_lo, rows, cols, row_frac, col_frac, weights):
     owners = rows.shape[0]
-    part = owners * 8
+    part = owners * 4
     lanes = iota((owners, part), 1)
-    owner_of = one_hot((lanes // 8) % owners == iota((owners, part), 0))
+    owner_of = one_hot(lanes // 4 == iota((owners, part), 0))
     spread = [dot(x, owner_of, ((0,), (0,))) for x in slots]
-    place = (iota((1, part), 1) % 8).astype(F32)
-    pick = jnp.concatenate([jnp.where(spread[q] == place + 8.0 * half, 1.0, 0.0) for q, half in pieces_of], axis=1)
+    place = (iota((1, part), 1) % 4).astype(F32)
+    pick = jnp.concatenate([jnp.where(spread[q] == place + 4.0 * quarter, 1.0, 0.0) for q, quarter in pieces_of], axis=1)
     present = jnp.sum(pick, axis=0, keepdims=True)
     total = pick.shape[1]
     owner_mask = jnp.concatenate([owner_of.astype(F32)] * len(pieces_of), axis=1)
@@ -104,8 +104,7 @@
 def column_table(number, tile, main, carry):
     one = jnp.ones((), BF16)
     zero = jnp.zeros((), BF16)
-    first = 2.0 * number if isinstance(number, int) else 2.0 * number.astype(F32)
-    is_tile = [jnp.where(tile == first + k, 1.0, 0.0).astype(BF16) if tile.dtype == F32 else jnp.where(tile == first + k, one, zero) for k in (-1, 0, 1)]
+    is_tile = [jnp.where(tile == float(2 * number + k), one, zero) for k in (-1, 0, 1)]
     parts = []
     for k in (0, 1):
         parts.append(main[:16] * is_tile[k + 1] + carry * is_tile[k])
@@ -119,11 +118,6 @@
     gather = one_hot(iota((count, x.shape[0]), 0) == iota((count, x.shape[0]), 1) // group)
     high, low = pieces(x)
     return dot(gather, high) + dot(gather, low)
-
-
-def to_blocks(value):
-    half = value.shape[1] // 2
-    return jnp.concatenate([value[:, :half], value[:, half:]], axis=0).T
 
 
 def field_block(scr, n):
@@ -167,11 +161,12 @@
     given = (order_hi, order_lo, rows, small_i[2], small_f[0], small_f[1], small_f[2])
     own_slots, own_many = owner_slots(slab, owned_rows)
     last_slots, last_many = owner_slots(slab - 1, owned_rows)
-    flag_ref[0] = (jnp.maximum(own_many, last_many) > 0.5).astype(jnp.int32)
-    meta = slot_fields(slab, (own_slots, last_slots), ((0, 0), (0, 1), (1, 1)), *given)
-    meta_ref[:, :count] = meta[:, :count]
-    meta_ref[:, count : count + skip] = jnp.zeros((16, skip), F32)
-    meta_ref[:, count + skip :] = meta[:, count:]
+    flag_ref[0] = (last_many > 8.0).astype(jnp.int32)
+    flag_ref[1] = (jnp.maximum(own_many, last_many) > 8.0).astype(jnp.int32)
+    flag_ref[2] = (jnp.maximum(own_many, last_many) > 12.0).astype(jnp.int32)
+    quarters = [(q, n) for q in (0, 1) for n in range(4)]
+    meta = slot_fields(slab, (own_slots, last_slots), quarters, *given)
+    meta_ref[...] = meta
     own_rows = jnp.sum(jnp.where(iota(owned_rows.shape, 0) == slab, owned_rows, 0).astype(F32), axis=0, keepdims=True)
     own = jnp.floor(own_rows * 0.25)
     on_last = jnp.where(own_rows - own * 4.0 == 3.0, 1.0, 0.0)
@@ -179,9 +174,11 @@
     before = (kind == kind.T) & (iota((LANES, LANES), 0) < iota((LANES, LANES), 1))
     rank = jnp.sum(jnp.where(before, 1.0, 0.0), axis=0, keepdims=True)
     rank = jnp.where(on_last > 0.5, SLOTS - 1.0 - rank, rank)
-    half = jnp.where(rank >= 8.0, 1.0, 0.0)
-    place_ref[...] = jnp.concatenate([own * 8.0 + rank - 8.0 * half, half] + [jnp.zeros_like(own)] * 6, axis=0)
-    near = meta[:, skip:]
+    quarter = jnp.floor(rank * 0.25)
+    pair = jnp.floor(rank * 0.125)
+    half = quarter - 2.0 * pair
+    place_ref[...] = jnp.concatenate([own * 8.0 + pair * 4.0 + rank - 4.0 * quarter, half] + [jnp.zeros_like(own)] * 6, axis=0)
+    near = jnp.concatenate([meta[:, skip:count], meta[:, count + skip :]], axis=1)
     main, carry, tile16 = column_parts(near)
     acc = jnp.zeros((256, count), F32)
     for c in range(chunks):
@@ -203,37 +200,32 @@
     nothing = jnp.zeros((64, skip), F32)
     give(nothing, nothing, part)
 
-    @pl.when(flag_ref[0] != 0)
-    def _():
-        order = small_i[0]
-        order_hi = order // LANES
-        order_lo = order % LANES
-        rows = small_i[1]
-        slots, _ = owner_slots(slab - 1, lookup_rows(order_hi, order_lo, rows))
-        given = (order_hi, order_lo, rows, small_i[2], small_f[0], small_f[1], small_f[2])
-        meta_ref[:, count : count + skip] = slot_fields(slab, (slots,), ((0, 0),), *given)
-        far = jnp.concatenate([meta_ref[:, :skip], meta_ref[:, count : count + skip]], axis=1)
-        far_main, far_carry, _ = column_parts(far)
-        far_tile = jnp.broadcast_to(far[:1], (16, count))
-
-        def step(n, acc):
-            return acc + dot(field_block(scr, n), column_table(n, far_tile, far_main, far_carry))
-
-        acc = lax.fori_loop(0, scr.shape[1] // 2, step, jnp.zeros((256, count), F32))
-        first = row_sum(acc * row_sides(far), 4)
-        give(first[:, :skip], first[:, skip:], jnp.concatenate([own_ref[...], last_ref[:, skip:]], axis=1))
-
-
-def rest_kernel(scr, meta_ref, part_ref):
-    meta = meta_ref[:, : part_ref.shape[1]]
+    for quarter in (1, 0):
+        lanes = slice(LANES * quarter, LANES * quarter + LANES)
+
+        @pl.when(flag_ref[2 - quarter] != 0)
+        def _():
+            far = jnp.concatenate([meta_ref[:, lanes], meta_ref[:, count + lanes.start : count + lanes.stop]], axis=1)
+            first = shared_parts(scr, far)
+            own, last = first[:, :LANES], first[:, LANES:]
+            last_ref[:, lanes] = last
+            same_ref[:, lanes] = jnp.where(even, own, last)
+            cross_ref[:, lanes] = jnp.where(even, last, own)
+
+
+def shared_parts(scr, meta):
     main, carry, tile16 = column_parts(meta)
-    sums = [jnp.zeros((128, part_ref.shape[1]), F32)] * 2
+    sums = [jnp.zeros((128, meta.shape[1]), F32)] * 2
     for n in range(scr.shape[1] // 2):
         block = field_block(scr, n)
         table = column_table(n, tile16, main, carry)
         for m in (0, 1):
             sums[m] = sums[m] + dot(block[128 * m : 128 * m + 128], table)
-    part_ref[...] = row_sum(jnp.concatenate(sums, axis=0) * row_sides(meta), 4)
+    return row_sum(jnp.concatenate(sums, axis=0) * row_sides(meta), 4)
+
+
+def rest_kernel(scr, meta_ref, part_ref):
+    part_ref[...] = shared_parts(scr, meta_ref[:, : part_ref.shape[1]])
 
 
 def combine_kernel(rest_ref, own_ref, last_ref, same_ref, cross_ref, meta_ref, at_ref, block_ref, trace_ref, src_ref):
@@ -248,8 +240,11 @@
     spread = jnp.concatenate([value, before], axis=1) * weight
     squares = jnp.sum(spread[:, :count] * value, axis=0, keepdims=True)
     trace = jnp.sum(squares, axis=1, keepdims=True)
-    lines = to_blocks(value)
-    block_ref[...] = lines
+    for pair in (0, 1):
+        quarters = [value[:, LANES * n : LANES * n + LANES] for n in (2 * pair, 2 * pair + 1)]
+        lines = jnp.concatenate(quarters, axis=0).T
+        for o in range(LANES // 4):
+            block_ref[8 * o + 4 * pair : 8 * o + 4 * pair + 4, :] = lines[4 * o : 4 * o + 4]
     trace_ref[...] = jnp.broadcast_to(trace, trace_ref.shape)
     repeat = one_hot(iota((256, 64), 0) // 4 == iota((256, 64), 1))
     tall = dot(repeat, spread.astype(BF16))
@@ -337,7 +332,7 @@
         forward_kernel,
         [("s", at)] + [("h", x) for x in flat] + [("h", fields)],
         [("w", (64, per_list), F32)] * 3
-        + [("w", (64, half), F32), ("w", (16, 2 * per_list), F32), ("w", (8, LANES), F32), ("s", (1,), jnp.int32)]
+        + [("w", (64, half), F32), ("w", (16, 2 * per_list), F32), ("w", (8, LANES), F32), ("s", (3,), jnp.int32)]
         + [("w", (16, tiles, 16, LANES), BF16)],
         [
             pltpu.VMEM((3, slabs, LANES), jnp.int32),

time: 49.4 us -> 40.7 us (0.82)
  starting transfers between devices: 27.1 us -> 18.2 us
    all_to_all x1, starting transfers between devices: 17.6 us -> 8.74 us  [body(): lax.all_to_all(send.reshape(slabs, 1, 9 * LANES), 'slab', 0, 0, tiled=True)]
  transfers between devices with their start and end apart: 6 -> 6, of which waited for: 4 -> 4; matrix products, arithmetic and copies ran while one was open for 0% -> 0% of each run, Pallas kernels for 13% -> 16%
where the time goes in v4:
time: 40.7 us; the launch traced here: 40.4 us
  starting transfers between devices  18.2 us (45%)
  Pallas kernels  13.8 us (34%)
  waiting for transfers between devices  7.65 us (19%)
  between operations  0.69 us (2%)
    pallas_call x6, Pallas kernels, call(): pl.pallas_call(functools.partial(kernel, **params), in_specs=[pl.BlockSpe...  13.8 us
    all_to_all x1, starting transfers between devices, body(): lax.all_to_all(send.reshape(slabs, 1, 9 * LANES), 'slab', 0, 0, tiled=True)  8.74 us
    ppermute x3, starting transfers between devices, body(): lax.ppermute(trace, 'probe', [(i, (i + k) % groups) for i in range(groups)])  4.91 us
    ppermute x3, waiting for transfers between devices, body(): lax.ppermute(trace, 'probe', [(i, (i + k) % groups) for i in range(groups)])  3.29 us
    ppermute x1, starting transfers between devices, body(): cross = lax.ppermute(to_cross, 'slab', swap_cross)  3.14 us
    all_to_all x1, waiting for transfers between devices, body(): lax.all_to_all(send.reshape(slabs, 1, 9 * LANES), 'slab', 0, 0, tiled=True)  2.66 us
    ppermute x1, waiting for transfers between devices, body(): cross = lax.ppermute(to_cross, 'slab', swap_cross)  1.7 us
    ppermute x1, starting transfers between devices, body(): same = lax.ppermute(to_same, 'slab', swap_same)  1.46 us
  transfers between devices with their start and end apart: 6, of which 4 were waited for; matrix products, arithmetic and copies ran while one was open for 0% of the time, Pallas kernels for 16%

profile of v4, /device:TPU:1, one launch (start us, length us, event | category | flops | bytes accessed | tf_op | source)
XLA Modules:
  0.0 40.4 jit_solution(14348599529327607814)
XLA Ops:
  0.6 5.4 %shard_map.94 = (f32[64,512]{1,0:T(8,128)S(1)}, f32[64,512]{1,0:T(8,128)S(1)}, f32[64,512]{1,0:T(8,128)S(1)}, f32[64,256]{1,0:T(8,128)S(1)}, f32[16,1024]{1,0:T(...) custom-call(s32[1]{0:T(128)} %bitcast.slab_ref.at_ref, s32[32,128]{1,0:T(8,128)} %bitcast.19, ...), custom_call_target="tpu_custom_call" | custom-call | tf_op jit(solution)/shard_map/pallas_call | solution.py:312
  6.1 1.5 %collective-permute-start = (f32[64,512]{1,0:T(8,128)S(1)}, f32[64,512]{1,0:T(8,128)S(1)}, u32[]{:S(2)}, u32[]{:S(2)}) collective-permute-start(f32[64,512]{1,0:T(8,128)S(1)} %get-tuple-element.20), channel_id=1, source_target_pairs={{0,4},{4,0},{8,12},{12,8},{16,20},{20,16},{24,28},{28,24},{32,36},... | collective-permute-start | bytes 393224 | tf_op jit(solution)/shard_map/ppermute | solution.py:347
  7.5 3.1 %collective-permute-start.1 = (f32[64,512]{1,0:T(8,128)S(1)}, f32[64,512]{1,0:T(8,128)S(1)}, u32[]{:S(2)}, u32[]{:S(2)}) collective-permute-start(f32[64,512]{1,0:T(8,128)S(1)} %get-tuple-element.21), channel_id=1, source_target_pairs={{4,8},{8,4},{12,16},{16,12},{20,24},{24,20},{28,32},{32,28},{36,40... | collective-permute-start | bytes 393224 | tf_op jit(solution)/shard_map/ppermute | solution.py:346
  10.7 1.4 %shard_map.95.rest_ref = f32[64,256]{1,0:T(8,128)S(1)} custom-call(bf16[16,64,16,128]{3,2,1,0:T(8,128)(2,1)S(1)} %get-tuple-element.16.scr, f32[16,1024]{1,0:T(8,128)S(1)} %get-tuple-element.17.meta_ref), custom_call_target="tpu_custom_call" | custom-call | tf_op jit(solution)/shard_map/pallas_call | solution.py:312
  12.1 0.0 collective-permute-done.same_ref
  12.1 1.7 %collective-permute-done.1.cross_ref = f32[64,512]{1,0:T(8,128)S(1)} collective-permute-done((f32[64,512]{1,0:T(8,128)S(1)}, f32[64,512]{1,0:T(8,128)S(1)}, u32[]{:S(2)}, u32[]{:S(2)}) %collective-permute-start.1) | collective-permute-done | bytes 131104 | tf_op jit(solution)/shard_map/ppermute | solution.py:346
  13.8 0.3 shard_map.96
  14.1 4.2 %collective-permute-start.4 = (f32[8,128]{1,0:T(8,128)S(1)}, f32[8,128]{1,0:T(8,128)S(1)}, u32[]{:S(2)}, u32[]{:S(2)}) collective-permute-start(f32[8,128]{1,0:T(8,128)S(1)} %get-tuple-element.25.refs_0_), channel_id=1, source_target_pairs={{0,3},{1,0},{2,1},{3,2},{4,7},{5,4},{6,5},{7,6},{8,11},{9,8},{10,9... | collective-permute-start | bytes 12296 | tf_op jit(solution)/shard_map/ppermute | solution.py:356
  18.4 0.0 collective-permute-start.3
  18.4 0.7 %collective-permute-start.2 = (f32[8,128]{1,0:T(8,128)S(1)}, f32[8,128]{1,0:T(8,128)S(1)}, u32[]{:S(2)}, u32[]{:S(2)}) collective-permute-start(f32[8,128]{1,0:T(8,128)S(1)} %get-tuple-element.25.refs_0_), channel_id=1, source_target_pairs={{0,1},{1,2},{2,3},{3,0},{4,5},{5,6},{6,7},{7,4},{8,9},{9,10},{10,1... | collective-permute-start | bytes 12296 | tf_op jit(solution)/shard_map/ppermute | solution.py:356
  19.0 0.1 collective-permute-done.4.refs_3_
  19.1 3.2 %collective-permute-done.3.refs_2_ = f32[8,128]{1,0:T(8,128)S(1)} collective-permute-done((f32[8,128]{1,0:T(8,128)S(1)}, f32[8,128]{1,0:T(8,128)S(1)}, u32[]{:S(2)}, u32[]{:S(2)}) %collective-permute-start.3) | collective-permute-done | bytes 4128 | tf_op jit(solution)/shard_map/ppermute | solution.py:356
  22.3 0.0 collective-permute-done.2.refs_1_
  22.3 0.7 %shard_map.98 = f32[288,128]{1,0:T(8,128)} custom-call(f32[256,128]{1,0:T(8,128)S(1)} %get-tuple-element.24.block_ref, f32[8,128]{1,0:T(8,128)S(1)} %get-tuple-element.25.refs_0_, f32[8,128]{1,0:T(8,128)S(1)} %collective-permute-done.2.refs_1_, f32[8,128]{1,0:T(8,128)S(1)} %collective-permute-done.3.refs_2_, f32[8,128]{1,0:T(8,128)S(1)} %collective-permute-done.4.refs_3_), custom_call_target="tpu_custom_call" | custom-call | tf_op jit(solution)/shard_map/pallas_call | solution.py:312
  23.0 8.7 %all-to-all-start = ((f32[32,1,1152]{2,1,0:T(1,128)}), f32[32,1,1152]{2,1,0:T(1,128)S(1)}, u32[]{:S(2)}, u32[]{:S(2)}) async-start(f32[32,1,1152]{2,1,0:T(1,128)} %bitcast.11), calls=%async_computation | async-start | bytes 294912 | tf_op jit(solution)/shard_map/all_to_all | solution.py:358
  31.7 5.1 %shard_map.97 = bf16[16,4,64,4,128]{4,3,2,1,0:T(4,128)(2,1)} custom-call(bf16[256,1024]{1,0:T(8,128)(2,1)S(1)} %get-tuple-element.22.src_ref, f32[16,1024]{1,0:T(8,128)S(1)} %get-tuple-element.17.meta_ref, s32[3]{0:T(128)S(1)} %get-tuple-element.23.flag_ref), custom_call_target="tpu_custom_call" | custom-call | tf_op jit(solution)/shard_map/pallas_call | solution.py:312
  36.8 2.7 %all-to-all-done = f32[32,1,1152]{2,1,0:T(1,128)S(1)} async-done(((f32[32,1,1152]{2,1,0:T(1,128)}), f32[32,1,1152]{2,1,0:T(1,128)S(1)}, u32[]{:S(2)}, u32[]{:S(2)}) %all-to-all-start) | async-done | bytes 147488 | tf_op jit(solution)/shard_map/all_to_all | solution.py:358
  39.5 0.9 %shard_map.99 = (f32[64,128]{1,0:T(8,128)}, f32[1,1]{1,0:T(1,128)}) custom-call(f32[288,128]{1,0:T(8,128)S(1)} %bitcast.16, f32[8,128]{1,0:T(8,128)S(1)} %get-tuple-element.26.place_ref), custom_call_target="tpu_custom_call" | custom-call | tf_op jit(solution)/shard_map/pallas_call | solution.py:312
Async XLA Ops:
  6.1 6.0 %collective-permute-start = (f32[64,512]{1,0:T(8,128)S(1)}, f32[64,512]{1,0:T(8,128)S(1)}, u32[]{:S(2)}, u32[]{:S(2)}) collective-permute-start(f32[64,512]{1,0:T(8,128)S(1)} %get-tuple-element.20), channel_id=1, source_target_pairs={{0,4},{4,0},{8,12},{12,8},{16,20},{20,16},{24,28},{28,24},{32,36},... | collective-permute-start | bytes 393224 | tf_op jit(solution)/shard_map/ppermute | solution.py:347
  7.5 6.3 %collective-permute-start.1 = (f32[64,512]{1,0:T(8,128)S(1)}, f32[64,512]{1,0:T(8,128)S(1)}, u32[]{:S(2)}, u32[]{:S(2)}) collective-permute-start(f32[64,512]{1,0:T(8,128)S(1)} %get-tuple-element.21), channel_id=1, source_target_pairs={{4,8},{8,4},{12,16},{16,12},{20,24},{24,20},{28,32},{32,28},{36,40... | collective-permute-start | bytes 393224 | tf_op jit(solution)/shard_map/ppermute | solution.py:346
  14.1 5.0 %collective-permute-start.4 = (f32[8,128]{1,0:T(8,128)S(1)}, f32[8,128]{1,0:T(8,128)S(1)}, u32[]{:S(2)}, u32[]{:S(2)}) collective-permute-start(f32[8,128]{1,0:T(8,128)S(1)} %get-tuple-element.25.refs_0_), channel_id=1, source_target_pairs={{0,3},{1,0},{2,1},{3,2},{4,7},{5,4},{6,5},{7,6},{8,11},{9,8},{10,9... | collective-permute-start | bytes 12296 | tf_op jit(solution)/shard_map/ppermute | solution.py:356
  18.4 4.0 %collective-permute-start.3 = (f32[8,128]{1,0:T(8,128)S(1)}, f32[8,128]{1,0:T(8,128)S(1)}, u32[]{:S(2)}, u32[]{:S(2)}) collective-permute-start(f32[8,128]{1,0:T(8,128)S(1)} %get-tuple-element.25.refs_0_), channel_id=1, source_target_pairs={{0,2},{1,3},{2,0},{3,1},{4,6},{5,7},{6,4},{7,5},{8,10},{9,11},{10,... | collective-permute-start | bytes 12296 | tf_op jit(solution)/shard_map/ppermute | solution.py:356
  18.4 4.0 %collective-permute-start.2 = (f32[8,128]{1,0:T(8,128)S(1)}, f32[8,128]{1,0:T(8,128)S(1)}, u32[]{:S(2)}, u32[]{:S(2)}) collective-permute-start(f32[8,128]{1,0:T(8,128)S(1)} %get-tuple-element.25.refs_0_), channel_id=1, source_target_pairs={{0,1},{1,2},{2,3},{3,0},{4,5},{5,6},{6,7},{7,4},{8,9},{9,10},{10,1... | collective-permute-start | bytes 12296 | tf_op jit(solution)/shard_map/ppermute | solution.py:356
  23.0 16.5 %all-to-all-start = ((f32[32,1,1152]{2,1,0:T(1,128)}), f32[32,1,1152]{2,1,0:T(1,128)S(1)}, u32[]{:S(2)}, u32[]{:S(2)}) async-start(f32[32,1,1152]{2,1,0:T(1,128)} %bitcast.11), calls=%async_computation | async-start | bytes 294912 | tf_op jit(solution)/shard_map/all_to_all | solution.py:358

commit v5 on v4

--- a/solution.py
+++ b/solution.py
@@ -14,6 +14,10 @@
 VMEM_LIMIT = 32 * 2**20
 CHUNKS = 2
 OUT_CHUNKS = 8
+
+
+def exchange_order(slabs):
+    return list(range(slabs // 2, slabs)) + list(range(slabs // 2))[::-1]
 
 
 def iota(shape, dim):
@@ -290,14 +294,15 @@
 def pack_kernel(block_ref, *refs):
     *trace_refs, send_ref = refs
     trace = sum(ref[...] for ref in trace_refs)[:1, :]
-    for o in range(block_ref.shape[0] // 8):
-        send_ref[9 * o : 9 * o + 8, :] = block_ref[8 * o : 8 * o + 8, :]
-        send_ref[9 * o + 8 : 9 * o + 9, :] = trace
+    for n, o in enumerate(exchange_order(block_ref.shape[0] // 8)):
+        send_ref[9 * n : 9 * n + 8, :] = block_ref[8 * o : 8 * o + 8, :]
+        send_ref[9 * n + 8 : 9 * n + 9, :] = trace
 
 
 def finish_kernel(got_ref, place_ref, observed_ref, total_ref, *, scale):
     slabs = got_ref.shape[0] // 9
-    values = jnp.concatenate([got_ref[9 * q : 9 * q + 8, :] for q in range(slabs)], axis=0)
+    blocks = {q: got_ref[9 * n : 9 * n + 8, :] for n, q in enumerate(exchange_order(slabs))}
+    values = jnp.concatenate([blocks[q] for q in range(slabs)], axis=0)
     pick = one_hot(iota((8 * slabs, LANES), 0).astype(F32) == place_ref[0:1, :])
     found = sum(dot(part, pick, ((0,), (0,))) for part in pieces(values))
     observed_ref[...] = jnp.where(place_ref[1:2, :] > 0.5, found[64:], found[:64])
@@ -355,7 +360,9 @@
     for k in range(1, groups):
         traces.append(lax.ppermute(trace, "probe", [(i, (i + k) % groups) for i in range(groups)]))
     (send,) = call(pack_kernel, [("w", blocks)] + [("w", x) for x in traces], [("w", (9 * slabs, LANES), F32)])
-    got = lax.all_to_all(send.reshape(slabs, 1, 9 * LANES), "slab", 0, 0, tiled=True)
+    got = lax.all_to_all(
+        send.reshape(slabs, 1, 9 * LANES), "slab", 0, 0, axis_index_groups=[exchange_order(slabs)], tiled=True
+    )
     (out,) = call(
         adjoint_kernel,
         [("w", sources), ("w", meta), ("s", flag)],

time: 40.7 us -> 39.7 us (0.975)
  waiting for transfers between devices: 7.65 us -> 5.17 us
  starting transfers between devices: 18.2 us -> 19.8 us
    all_to_all x1, waiting for transfers between devices: 2.66 us -> 0.18 us  [body(): lax.all_to_all(send.reshape(slabs, 1, 9 * LANES), 'slab', 0, 0, axis_inde...]
    all_to_all x1, starting transfers between devices: 8.74 us -> 10.3 us  [body(): lax.all_to_all(send.reshape(slabs, 1, 9 * LANES), 'slab', 0, 0, axis_inde...]
  transfers between devices with their start and end apart: 6 -> 6, of which waited for: 4 -> 4; matrix products, arithmetic and copies ran while one was open for 0% -> 0% of each run, Pallas kernels for 16% -> 17%
where the time goes in v5:
time: 39.7 us; the launch traced here: 39.4 us
  starting transfers between devices  19.8 us (50%)
  Pallas kernels  13.8 us (35%)
  waiting for transfers between devices  5.17 us (13%)
  between operations  0.69 us (2%)
    pallas_call x6, Pallas kernels, call(): pl.pallas_call(functools.partial(kernel, **params), in_specs=[pl.BlockSpe...  13.8 us
    all_to_all x1, starting transfers between devices, body(): lax.all_to_all(send.reshape(slabs, 1, 9 * LANES), 'slab', 0, 0, axis_inde...  10.3 us
    ppermute x3, starting transfers between devices, body(): lax.ppermute(trace, 'probe', [(i, (i + k) % groups) for i in range(groups)])  4.91 us
    ppermute x3, waiting for transfers between devices, body(): lax.ppermute(trace, 'probe', [(i, (i + k) % groups) for i in range(groups)])  3.29 us
    ppermute x1, starting transfers between devices, body(): cross = lax.ppermute(to_cross, 'slab', swap_cross)  3.14 us
    ppermute x1, waiting for transfers between devices, body(): cross = lax.ppermute(to_cross, 'slab', swap_cross)  1.7 us
    ppermute x1, starting transfers between devices, body(): same = lax.ppermute(to_same, 'slab', swap_same)  1.46 us
  transfers between devices with their start and end apart: 6, of which 4 were waited for; matrix products, arithmetic and copies ran while one was open for 0% of the time, Pallas kernels for 17%

profile of v5, /device:TPU:1, one launch (start us, length us, event | category | flops | bytes accessed | tf_op | source)
XLA Modules:
  0.0 39.4 jit_solution(3956687654261078606)
XLA Ops:
  0.6 5.4 %shard_map.94 = (f32[64,512]{1,0:T(8,128)S(1)}, f32[64,512]{1,0:T(8,128)S(1)}, f32[64,512]{1,0:T(8,128)S(1)}, f32[64,256]{1,0:T(8,128)S(1)}, f32[16,1024]{1,0:T(...) custom-call(s32[1]{0:T(128)} %bitcast.slab_ref.at_ref, s32[32,128]{1,0:T(8,128)} %bitcast.19, ...), custom_call_target="tpu_custom_call" | custom-call | tf_op jit(solution)/shard_map/pallas_call | solution.py:317
  6.1 1.5 %collective-permute-start = (f32[64,512]{1,0:T(8,128)S(1)}, f32[64,512]{1,0:T(8,128)S(1)}, u32[]{:S(2)}, u32[]{:S(2)}) collective-permute-start(f32[64,512]{1,0:T(8,128)S(1)} %get-tuple-element.20), channel_id=1, source_target_pairs={{0,4},{4,0},{8,12},{12,8},{16,20},{20,16},{24,28},{28,24},{32,36},... | collective-permute-start | bytes 393224 | tf_op jit(solution)/shard_map/ppermute | solution.py:352
  7.5 3.1 %collective-permute-start.1 = (f32[64,512]{1,0:T(8,128)S(1)}, f32[64,512]{1,0:T(8,128)S(1)}, u32[]{:S(2)}, u32[]{:S(2)}) collective-permute-start(f32[64,512]{1,0:T(8,128)S(1)} %get-tuple-element.21), channel_id=1, source_target_pairs={{4,8},{8,4},{12,16},{16,12},{20,24},{24,20},{28,32},{32,28},{36,40... | collective-permute-start | bytes 393224 | tf_op jit(solution)/shard_map/ppermute | solution.py:351
  10.7 1.4 %shard_map.95.rest_ref = f32[64,256]{1,0:T(8,128)S(1)} custom-call(bf16[16,64,16,128]{3,2,1,0:T(8,128)(2,1)S(1)} %get-tuple-element.16.scr, f32[16,1024]{1,0:T(8,128)S(1)} %get-tuple-element.17.meta_ref), custom_call_target="tpu_custom_call" | custom-call | tf_op jit(solution)/shard_map/pallas_call | solution.py:317
  12.1 0.0 collective-permute-done.same_ref
  12.1 1.7 %collective-permute-done.1.cross_ref = f32[64,512]{1,0:T(8,128)S(1)} collective-permute-done((f32[64,512]{1,0:T(8,128)S(1)}, f32[64,512]{1,0:T(8,128)S(1)}, u32[]{:S(2)}, u32[]{:S(2)}) %collective-permute-start.1) | collective-permute-done | bytes 131104 | tf_op jit(solution)/shard_map/ppermute | solution.py:351
  13.8 0.3 shard_map.96
  14.1 4.2 %collective-permute-start.4 = (f32[8,128]{1,0:T(8,128)S(1)}, f32[8,128]{1,0:T(8,128)S(1)}, u32[]{:S(2)}, u32[]{:S(2)}) collective-permute-start(f32[8,128]{1,0:T(8,128)S(1)} %get-tuple-element.25.refs_0_), channel_id=1, source_target_pairs={{0,3},{1,0},{2,1},{3,2},{4,7},{5,4},{6,5},{7,6},{8,11},{9,8},{10,9... | collective-permute-start | bytes 12296 | tf_op jit(solution)/shard_map/ppermute | solution.py:361
  18.4 0.0 collective-permute-start.3
  18.4 0.7 %collective-permute-start.2 = (f32[8,128]{1,0:T(8,128)S(1)}, f32[8,128]{1,0:T(8,128)S(1)}, u32[]{:S(2)}, u32[]{:S(2)}) collective-permute-start(f32[8,128]{1,0:T(8,128)S(1)} %get-tuple-element.25.refs_0_), channel_id=1, source_target_pairs={{0,1},{1,2},{2,3},{3,0},{4,5},{5,6},{6,7},{7,4},{8,9},{9,10},{10,1... | collective-permute-start | bytes 12296 | tf_op jit(solution)/shard_map/ppermute | solution.py:361
  19.0 0.1 collective-permute-done.4.refs_3_
  19.1 3.2 %collective-permute-done.3.refs_2_ = f32[8,128]{1,0:T(8,128)S(1)} collective-permute-done((f32[8,128]{1,0:T(8,128)S(1)}, f32[8,128]{1,0:T(8,128)S(1)}, u32[]{:S(2)}, u32[]{:S(2)}) %collective-permute-start.3) | collective-permute-done | bytes 4128 | tf_op jit(solution)/shard_map/ppermute | solution.py:361
  22.3 0.0 collective-permute-done.2.refs_1_
  22.3 0.7 %shard_map.98 = f32[288,128]{1,0:T(8,128)} custom-call(f32[256,128]{1,0:T(8,128)S(1)} %get-tuple-element.24.block_ref, f32[8,128]{1,0:T(8,128)S(1)} %get-tuple-element.25.refs_0_, f32[8,128]{1,0:T(8,128)S(1)} %collective-permute-done.2.refs_1_, f32[8,128]{1,0:T(8,128)S(1)} %collective-permute-done.3.refs_2_, f32[8,128]{1,0:T(8,128)S(1)} %collective-permute-done.4.refs_3_), custom_call_target="tpu_custom_call" | custom-call | tf_op jit(solution)/shard_map/pallas_call | solution.py:317
  23.0 10.3 %all-to-all-start = ((f32[32,1,1152]{2,1,0:T(1,128)}), f32[32,1,1152]{2,1,0:T(1,128)S(1)}, u32[]{:S(2)}, u32[]{:S(2)}) async-start(f32[32,1,1152]{2,1,0:T(1,128)} %bitcast.11), calls=%async_computation | async-start | bytes 294912 | tf_op jit(solution)/shard_map/all_to_all | solution.py:363
  33.3 5.1 %shard_map.97 = bf16[16,4,64,4,128]{4,3,2,1,0:T(4,128)(2,1)} custom-call(bf16[256,1024]{1,0:T(8,128)(2,1)S(1)} %get-tuple-element.22.src_ref, f32[16,1024]{1,0:T(8,128)S(1)} %get-tuple-element.17.meta_ref, s32[3]{0:T(128)S(1)} %get-tuple-element.23.flag_ref), custom_call_target="tpu_custom_call" | custom-call | tf_op jit(solution)/shard_map/pallas_call | solution.py:317
  38.4 0.2 all-to-all-done
  38.6 0.8 %shard_map.99 = (f32[64,128]{1,0:T(8,128)}, f32[1,1]{1,0:T(1,128)}) custom-call(f32[288,128]{1,0:T(8,128)S(1)} %bitcast.16, f32[8,128]{1,0:T(8,128)S(1)} %get-tuple-element.26.place_ref), custom_call_target="tpu_custom_call" | custom-call | tf_op jit(solution)/shard_map/pallas_call | solution.py:317
Async XLA Ops:
  6.1 6.0 %collective-permute-start = (f32[64,512]{1,0:T(8,128)S(1)}, f32[64,512]{1,0:T(8,128)S(1)}, u32[]{:S(2)}, u32[]{:S(2)}) collective-permute-start(f32[64,512]{1,0:T(8,128)S(1)} %get-tuple-element.20), channel_id=1, source_target_pairs={{0,4},{4,0},{8,12},{12,8},{16,20},{20,16},{24,28},{28,24},{32,36},... | collective-permute-start | bytes 393224 | tf_op jit(solution)/shard_map/ppermute | solution.py:352
  7.5 6.3 %collective-permute-start.1 = (f32[64,512]{1,0:T(8,128)S(1)}, f32[64,512]{1,0:T(8,128)S(1)}, u32[]{:S(2)}, u32[]{:S(2)}) collective-permute-start(f32[64,512]{1,0:T(8,128)S(1)} %get-tuple-element.21), channel_id=1, source_target_pairs={{4,8},{8,4},{12,16},{16,12},{20,24},{24,20},{28,32},{32,28},{36,40... | collective-permute-start | bytes 393224 | tf_op jit(solution)/shard_map/ppermute | solution.py:351
  14.1 5.0 %collective-permute-start.4 = (f32[8,128]{1,0:T(8,128)S(1)}, f32[8,128]{1,0:T(8,128)S(1)}, u32[]{:S(2)}, u32[]{:S(2)}) collective-permute-start(f32[8,128]{1,0:T(8,128)S(1)} %get-tuple-element.25.refs_0_), channel_id=1, source_target_pairs={{0,3},{1,0},{2,1},{3,2},{4,7},{5,4},{6,5},{7,6},{8,11},{9,8},{10,9... | collective-permute-start | bytes 12296 | tf_op jit(solution)/shard_map/ppermute | solution.py:361
  18.4 4.0 %collective-permute-start.3 = (f32[8,128]{1,0:T(8,128)S(1)}, f32[8,128]{1,0:T(8,128)S(1)}, u32[]{:S(2)}, u32[]{:S(2)}) collective-permute-start(f32[8,128]{1,0:T(8,128)S(1)} %get-tuple-element.25.refs_0_), channel_id=1, source_target_pairs={{0,2},{1,3},{2,0},{3,1},{4,6},{5,7},{6,4},{7,5},{8,10},{9,11},{10,... | collective-permute-start | bytes 12296 | tf_op jit(solution)/shard_map/ppermute | solution.py:361
  18.4 4.0 %collective-permute-start.2 = (f32[8,128]{1,0:T(8,128)S(1)}, f32[8,128]{1,0:T(8,128)S(1)}, u32[]{:S(2)}, u32[]{:S(2)}) collective-permute-start(f32[8,128]{1,0:T(8,128)S(1)} %get-tuple-element.25.refs_0_), channel_id=1, source_target_pairs={{0,1},{1,2},{2,3},{3,0},{4,5},{5,6},{6,7},{7,4},{8,9},{9,10},{10,1... | collective-permute-start | bytes 12296 | tf_op jit(solution)/shard_map/ppermute | solution.py:361
  23.0 15.6 %all-to-all-start = ((f32[32,1,1152]{2,1,0:T(1,128)}), f32[32,1,1152]{2,1,0:T(1,128)S(1)}, u32[]{:S(2)}, u32[]{:S(2)}) async-start(f32[32,1,1152]{2,1,0:T(1,128)} %bitcast.11), calls=%async_computation | async-start | bytes 294912 | tf_op jit(solution)/shard_map/all_to_all | solution.py:363

commit v6 on v5

--- a/solution.py
+++ b/solution.py
@@ -130,7 +130,7 @@
 
 def forward_kernel(
     slab_ref, rows_hbm, cols_hbm, rf_hbm, cf_hbm, w_hbm, order_hbm, u_ref,
-    last_ref, same_ref, cross_ref, own_ref, meta_ref, place_ref, flag_ref, scr,
+    cross_ref, meta_ref, place_ref, flag_ref, scr,
     small_i, small_f, sem, small_sem,
 ):
     chunks = CHUNKS
@@ -160,7 +160,7 @@
     order_lo = order % LANES
     rows = small_i[1]
     owned_rows = lookup_rows(order_hi, order_lo, rows)
-    count = last_ref.shape[1]
+    count = cross_ref.shape[1]
     skip = count // 2
     given = (order_hi, order_lo, rows, small_i[2], small_f[0], small_f[1], small_f[2])
     own_slots, own_many = owner_slots(slab, owned_rows)
@@ -168,6 +168,7 @@
     flag_ref[0] = (last_many > 8.0).astype(jnp.int32)
     flag_ref[1] = (jnp.maximum(own_many, last_many) > 8.0).astype(jnp.int32)
     flag_ref[2] = (jnp.maximum(own_many, last_many) > 12.0).astype(jnp.int32)
+    flag_ref[3] = slab % 2
     quarters = [(q, n) for q in (0, 1) for n in range(4)]
     meta = slot_fields(slab, (own_slots, last_slots), quarters, *given)
     meta_ref[...] = meta
@@ -182,39 +183,23 @@
     pair = jnp.floor(rank * 0.125)
     half = quarter - 2.0 * pair
     place_ref[...] = jnp.concatenate([own * 8.0 + pair * 4.0 + rank - 4.0 * quarter, half] + [jnp.zeros_like(own)] * 6, axis=0)
-    near = jnp.concatenate([meta[:, skip:count], meta[:, count + skip :]], axis=1)
-    main, carry, tile16 = column_parts(near)
-    acc = jnp.zeros((256, count), F32)
-    for c in range(chunks):
-        for k in range(4):
-            copy(c, k).wait()
-        for n in range(c * width // 2, (c + 1) * width // 2):
-            acc = acc + dot(field_block(scr, n), column_table(n, tile16, main, carry))
-    part = row_sum(acc * row_sides(near), 4)
-    even = slab % 2 == 0
-    own_ref[...] = part[:, :skip]
-
-    def give(own_first, last_first, part):
-        own = jnp.concatenate([own_first, part[:, :skip]], axis=1)
-        last = jnp.concatenate([last_first, part[:, skip:]], axis=1)
-        last_ref[...] = last
-        same_ref[...] = jnp.where(even, own, last)
-        cross_ref[...] = jnp.where(even, last, own)
-
-    nothing = jnp.zeros((64, skip), F32)
-    give(nothing, nothing, part)
-
+    near = jnp.where(slab % 2 == 0, meta[:, count + skip :], meta[:, skip:count])
+    for k in range(4 * chunks):
+        copy(k // 4, k % 4).wait()
+    cross_ref[:, :skip] = jnp.zeros((64, skip), F32)
+    cross_ref[:, skip:] = shared_parts(scr, near)
+    far_parts(scr, meta_ref, flag_ref, cross_ref, 0)
+
+
+def far_parts(scr, meta_ref, flag_ref, part_ref, parity):
+    count = part_ref.shape[1]
     for quarter in (1, 0):
         lanes = slice(LANES * quarter, LANES * quarter + LANES)
 
         @pl.when(flag_ref[2 - quarter] != 0)
         def _():
-            far = jnp.concatenate([meta_ref[:, lanes], meta_ref[:, count + lanes.start : count + lanes.stop]], axis=1)
-            first = shared_parts(scr, far)
-            own, last = first[:, :LANES], first[:, LANES:]
-            last_ref[:, lanes] = last
-            same_ref[:, lanes] = jnp.where(even, own, last)
-            cross_ref[:, lanes] = jnp.where(even, last, own)
+            own, last = meta_ref[:, lanes], meta_ref[:, count + lanes.start : count + lanes.stop]
+            part_ref[:, lanes] = shared_parts(scr, jnp.where(flag_ref[3] == parity, last, own))
 
 
 def shared_parts(scr, meta):
@@ -228,18 +213,32 @@
     return row_sum(jnp.concatenate(sums, axis=0) * row_sides(meta), 4)
 
 
-def rest_kernel(scr, meta_ref, part_ref):
-    part_ref[...] = shared_parts(scr, meta_ref[:, : part_ref.shape[1]])
-
-
-def combine_kernel(rest_ref, own_ref, last_ref, same_ref, cross_ref, meta_ref, at_ref, block_ref, trace_ref, src_ref):
-    count = last_ref.shape[1]
+def rest_kernel(scr, meta_ref, flag_ref, same_ref, part_ref):
+    count = same_ref.shape[1]
+    skip = count // 2
+    near = jnp.where(flag_ref[3] == 1, meta_ref[:, count + skip :], meta_ref[:, skip:count])
+    meta = jnp.concatenate([near, meta_ref[:, :skip]], axis=1)
+    main, carry, tile16 = column_parts(meta)
+    acc = jnp.zeros((256, count), F32)
+    for n in range(scr.shape[1] // 2):
+        acc = acc + dot(field_block(scr, n), column_table(n, tile16, main, carry))
+    part = row_sum(acc * row_sides(meta), 4)
+    part_ref[...] = part[:, skip:]
+    same_ref[:, :skip] = jnp.zeros((64, skip), F32)
+    same_ref[:, skip:] = part[:, :skip]
+    far_parts(scr, meta_ref, flag_ref, same_ref, 1)
+
+
+def combine_kernel(rest_ref, to_same_ref, to_cross_ref, same_ref, cross_ref, meta_ref, at_ref, block_ref, trace_ref, src_ref):
+    count = same_ref.shape[1]
     even = at_ref[0] % 2 == 0
-    own = jnp.concatenate([rest_ref[...], own_ref[...]], axis=1)
     same = same_ref[...]
     cross = cross_ref[...]
+    to_same = to_same_ref[...]
+    to_cross = to_cross_ref[...]
+    own = jnp.concatenate([rest_ref[...], jnp.where(even, to_same, to_cross)[:, count // 2 :]], axis=1)
     value = own + jnp.where(even, same, cross)
-    before = last_ref[...] + jnp.where(even, cross, same)
+    before = jnp.where(even, to_cross + cross, to_same + same)
     weight = meta_ref[8:9, :]
     spread = jnp.concatenate([value, before], axis=1) * weight
     squares = jnp.sum(spread[:, :count] * value, axis=0, keepdims=True)
@@ -333,11 +332,10 @@
     fields = probe_fields.reshape(16, 4, 4, tiles, LANES).transpose(0, 1, 3, 2, 4)
     flat = [x.reshape(slabs, LANES) for x in (sensor_rows, sensor_cols, row_frac, col_frac, sensor_weights, owner_order)]
     half = per_list // 2
-    last, to_same, to_cross, own, meta, place, flag, lines = call(
+    to_cross, meta, place, flag, lines = call(
         forward_kernel,
         [("s", at)] + [("h", x) for x in flat] + [("h", fields)],
-        [("w", (64, per_list), F32)] * 3
-        + [("w", (64, half), F32), ("w", (16, 2 * per_list), F32), ("w", (8, LANES), F32), ("s", (3,), jnp.int32)]
+        [("w", (64, per_list), F32), ("w", (16, 2 * per_list), F32), ("w", (8, LANES), F32), ("s", (4,), jnp.int32)]
         + [("w", (16, tiles, 16, LANES), BF16)],
         [
             pltpu.VMEM((3, slabs, LANES), jnp.int32),
@@ -349,11 +347,15 @@
     swap_cross = [(i, i + 1 if i % 2 else i - 1) for i in range(1, slabs - 1)]
     swap_same = [(i, i - 1 if i % 2 else i + 1) for i in range(slabs)]
     cross = lax.ppermute(to_cross, "slab", swap_cross)
+    to_same, rest = call(
+        rest_kernel,
+        [("w", lines), ("w", meta), ("s", flag)],
+        [("w", (64, per_list), F32), ("w", (64, half), F32)],
+    )
     same = lax.ppermute(to_same, "slab", swap_same)
-    (rest,) = call(rest_kernel, [("w", lines), ("w", meta)], [("w", (64, half), F32)])
     blocks, trace, sources = call(
         combine_kernel,
-        [("w", rest), ("w", own), ("w", last), ("w", same), ("w", cross), ("w", meta), ("s", at)],
+        [("w", x) for x in (rest, to_same, to_cross, same, cross, meta)] + [("s", at)],
         [("w", (8 * slabs, LANES), F32), ("w", (8, LANES), F32), ("w", (256, 2 * per_list), BF16)],
     )
     traces = [trace]

time: 39.7 us -> 43.2 us (1.088)
  starting transfers between devices: 19.8 us -> 21.2 us
  waiting for transfers between devices: 5.17 us -> 6.4 us
  Pallas kernels: 13.8 us -> 14.6 us
    ppermute x1, waiting for transfers between devices: 1.7 us -> 3.13 us  [body(): cross = lax.ppermute(to_cross, 'slab', swap_cross)]
    all_to_all x1, starting transfers between devices: 10.3 us -> 11.7 us  [body(): lax.all_to_all(send.reshape(slabs, 1, 9 * LANES), 'slab', 0, 0, axis_inde...]
    pallas_call x6, Pallas kernels: 13.8 us -> 14.6 us  [call(): pl.pallas_call(functools.partial(kernel, **params), in_specs=[pl.BlockSpe...]
  transfers between devices with their start and end apart: 6 -> 6, of which waited for: 4 -> 3; matrix products, arithmetic and copies ran while one was open for 0% -> 0% of each run, Pallas kernels for 17% -> 12%
where the time goes in v6:
time: 43.2 us; the launch traced here: 42.9 us
  starting transfers between devices  21.2 us (49%)
  Pallas kernels  14.6 us (34%)
  waiting for transfers between devices  6.4 us (15%)
  between operations  0.7 us (2%)
    pallas_call x6, Pallas kernels, call(): pl.pallas_call(functools.partial(kernel, **params), in_specs=[pl.BlockSpe...  14.6 us
    all_to_all x1, starting transfers between devices, body(): lax.all_to_all(send.reshape(slabs, 1, 9 * LANES), 'slab', 0, 0, axis_inde...  11.7 us
    ppermute x3, starting transfers between devices, body(): lax.ppermute(trace, 'probe', [(i, (i + k) % groups) for i in range(groups)])  4.93 us
    ppermute x3, waiting for transfers between devices, body(): lax.ppermute(trace, 'probe', [(i, (i + k) % groups) for i in range(groups)])  3.27 us
    ppermute x1, starting transfers between devices, body(): cross = lax.ppermute(to_cross, 'slab', swap_cross)  3.13 us
    ppermute x1, waiting for transfers between devices, body(): cross = lax.ppermute(to_cross, 'slab', swap_cross)  3.13 us
    ppermute x1, starting transfers between devices, body(): same = lax.ppermute(to_same, 'slab', swap_same)  1.46 us
  transfers between devices with their start and end apart: 6, of which 3 were waited for; matrix products, arithmetic and copies ran while one was open for 0% of the time, Pallas kernels for 12%

profile of v6, /device:TPU:1, one launch (start us, length us, event | category | flops | bytes accessed | tf_op | source)
XLA Modules:
  0.0 42.9 jit_solution(4474948603897054366)
XLA Ops:
  0.6 4.4 %shard_map.94 = (f32[64,512]{1,0:T(8,128)S(1)}, f32[16,1024]{1,0:T(8,128)S(1)}, f32[8,128]{1,0:T(8,128)S(1)}, s32[4]{0:T(128)S(1)}, bf16[16,64,16,128]{3,2,1,0:T(8,128)(2,1)S(1)}) custom-call(s32[1]{0:T(128)} %bitcast.slab_ref.at_ref, s32[32,128]{1,0:T(8,128)} %bitcast.19, s32[32,128]{1,0:T(8,128)} %bitcast.20, f32[32,128]{1,0:T(8,128)} %bitcast.21, ...), custom_call_target="tpu_custom_call" | custom-call | tf_op jit(solution)/shard_map/pallas_call | solution.py:316
  5.0 3.1 %shard_map.95 = (f32[64,512]{1,0:T(8,128)S(1)}, f32[64,256]{1,0:T(8,128)S(1)}) custom-call(bf16[16,64,16,128]{3,2,1,0:T(8,128)(2,1)S(1)} %get-tuple-element.15.scr, f32[16,1024]{1,0:T(8,128)S(1)} %get-tuple-element.16.meta_ref, s32[4]{0:T(128)S(1)} %get-tuple-element.17.flag_ref), custom_call_target="tpu_custom_call" | custom-call | tf_op jit(solution)/shard_map/pallas_call | solution.py:316
  8.1 1.5 %collective-permute-start = (f32[64,512]{1,0:T(8,128)S(1)}, f32[64,512]{1,0:T(8,128)S(1)}, u32[]{:S(2)}, u32[]{:S(2)}) collective-permute-start(f32[64,512]{1,0:T(8,128)S(1)} %get-tuple-element.19.to_same_ref), channel_id=1, source_target_pairs={{0,4},{4,0},{8,12},{12,8},{16,20},{20,16},{24,28},{28,24},{32,36},... | collective-permute-start | bytes 393224 | tf_op jit(solution)/shard_map/ppermute | solution.py:355
  9.6 3.1 %collective-permute-start.1 = (f32[64,512]{1,0:T(8,128)S(1)}, f32[64,512]{1,0:T(8,128)S(1)}, u32[]{:S(2)}, u32[]{:S(2)}) collective-permute-start(f32[64,512]{1,0:T(8,128)S(1)} %get-tuple-element.20.to_cross_ref), channel_id=1, source_target_pairs={{4,8},{8,4},{12,16},{16,12},{20,24},{24,20},{28,32},{32,28},{36,40... | collective-permute-start | bytes 393224 | tf_op jit(solution)/shard_map/ppermute | solution.py:349
  12.7 0.0 collective-permute-done.same_ref
  12.8 3.1 %collective-permute-done.1.cross_ref = f32[64,512]{1,0:T(8,128)S(1)} collective-permute-done((f32[64,512]{1,0:T(8,128)S(1)}, f32[64,512]{1,0:T(8,128)S(1)}, u32[]{:S(2)}, u32[]{:S(2)}) %collective-permute-start.1) | collective-permute-done | bytes 131104 | tf_op jit(solution)/shard_map/ppermute | solution.py:349
  15.9 0.3 shard_map.96
  16.2 4.2 %collective-permute-start.4 = (f32[8,128]{1,0:T(8,128)S(1)}, f32[8,128]{1,0:T(8,128)S(1)}, u32[]{:S(2)}, u32[]{:S(2)}) collective-permute-start(f32[8,128]{1,0:T(8,128)S(1)} %get-tuple-element.23.refs_0_), channel_id=1, source_target_pairs={{0,3},{1,0},{2,1},{3,2},{4,7},{5,4},{6,5},{7,6},{8,11},{9,8},{10,9... | collective-permute-start | bytes 12296 | tf_op jit(solution)/shard_map/ppermute | solution.py:363
  20.4 0.0 collective-permute-start.3
  20.4 0.7 %collective-permute-start.2 = (f32[8,128]{1,0:T(8,128)S(1)}, f32[8,128]{1,0:T(8,128)S(1)}, u32[]{:S(2)}, u32[]{:S(2)}) collective-permute-start(f32[8,128]{1,0:T(8,128)S(1)} %get-tuple-element.23.refs_0_), channel_id=1, source_target_pairs={{0,1},{1,2},{2,3},{3,0},{4,5},{5,6},{6,7},{7,4},{8,9},{9,10},{10,1... | collective-permute-start | bytes 12296 | tf_op jit(solution)/shard_map/ppermute | solution.py:363
  21.1 0.1 collective-permute-done.4.refs_3_
  21.2 3.2 %collective-permute-done.3.refs_2_ = f32[8,128]{1,0:T(8,128)S(1)} collective-permute-done((f32[8,128]{1,0:T(8,128)S(1)}, f32[8,128]{1,0:T(8,128)S(1)}, u32[]{:S(2)}, u32[]{:S(2)}) %collective-permute-start.3) | collective-permute-done | bytes 4128 | tf_op jit(solution)/shard_map/ppermute | solution.py:363
  24.4 0.0 collective-permute-done.2.refs_1_
  24.4 0.7 %shard_map.98 = f32[288,128]{1,0:T(8,128)} custom-call(f32[256,128]{1,0:T(8,128)S(1)} %get-tuple-element.22.block_ref, f32[8,128]{1,0:T(8,128)S(1)} %get-tuple-element.23.refs_0_, f32[8,128]{1,0:T(8,128)S(1)} %collective-permute-done.2.refs_1_, f32[8,128]{1,0:T(8,128)S(1)} %collective-permute-done.3.refs_2_, f32[8,128]{1,0:T(8,128)S(1)} %collective-permute-done.4.refs_3_), custom_call_target="tpu_custom_call" | custom-call | tf_op jit(solution)/shard_map/pallas_call | solution.py:316
  25.1 11.7 %all-to-all-start = ((f32[32,1,1152]{2,1,0:T(1,128)}), f32[32,1,1152]{2,1,0:T(1,128)S(1)}, u32[]{:S(2)}, u32[]{:S(2)}) async-start(f32[32,1,1152]{2,1,0:T(1,128)} %bitcast.11), calls=%async_computation | async-start | bytes 294912 | tf_op jit(solution)/shard_map/all_to_all | solution.py:365
  36.8 5.3 %shard_map.97 = bf16[16,4,64,4,128]{4,3,2,1,0:T(4,128)(2,1)} custom-call(bf16[256,1024]{1,0:T(8,128)(2,1)S(1)} %get-tuple-element.21.src_ref, f32[16,1024]{1,0:T(8,128)S(1)} %get-tuple-element.16.meta_ref, s32[4]{0:T(128)S(1)} %get-tuple-element.17.flag_ref), custom_call_target="tpu_custom_call" | custom-call | tf_op jit(solution)/shard_map/pallas_call | solution.py:316
  42.1 0.0 all-to-all-done
  42.1 0.9 %shard_map.99 = (f32[64,128]{1,0:T(8,128)}, f32[1,1]{1,0:T(1,128)}) custom-call(f32[288,128]{1,0:T(8,128)S(1)} %bitcast.16, f32[8,128]{1,0:T(8,128)S(1)} %get-tuple-element.24.place_ref), custom_call_target="tpu_custom_call" | custom-call | tf_op jit(solution)/shard_map/pallas_call | solution.py:316
Async XLA Ops:
  8.1 4.6 %collective-permute-start = (f32[64,512]{1,0:T(8,128)S(1)}, f32[64,512]{1,0:T(8,128)S(1)}, u32[]{:S(2)}, u32[]{:S(2)}) collective-permute-start(f32[64,512]{1,0:T(8,128)S(1)} %get-tuple-element.19.to_same_ref), channel_id=1, source_target_pairs={{0,4},{4,0},{8,12},{12,8},{16,20},{20,16},{24,28},{28,24},{32,36},... | collective-permute-start | bytes 393224 | tf_op jit(solution)/shard_map/ppermute | solution.py:355
  9.6 6.3 %collective-permute-start.1 = (f32[64,512]{1,0:T(8,128)S(1)}, f32[64,512]{1,0:T(8,128)S(1)}, u32[]{:S(2)}, u32[]{:S(2)}) collective-permute-start(f32[64,512]{1,0:T(8,128)S(1)} %get-tuple-element.20.to_cross_ref), channel_id=1, source_target_pairs={{4,8},{8,4},{12,16},{16,12},{20,24},{24,20},{28,32},{32,28},{36,40... | collective-permute-start | bytes 393224 | tf_op jit(solution)/shard_map/ppermute | solution.py:349
  16.2 5.0 %collective-permute-start.4 = (f32[8,128]{1,0:T(8,128)S(1)}, f32[8,128]{1,0:T(8,128)S(1)}, u32[]{:S(2)}, u32[]{:S(2)}) collective-permute-start(f32[8,128]{1,0:T(8,128)S(1)} %get-tuple-element.23.refs_0_), channel_id=1, source_target_pairs={{0,3},{1,0},{2,1},{3,2},{4,7},{5,4},{6,5},{7,6},{8,11},{9,8},{10,9... | collective-permute-start | bytes 12296 | tf_op jit(solution)/shard_map/ppermute | solution.py:363
  20.4 4.0 %collective-permute-start.3 = (f32[8,128]{1,0:T(8,128)S(1)}, f32[8,128]{1,0:T(8,128)S(1)}, u32[]{:S(2)}, u32[]{:S(2)}) collective-permute-start(f32[8,128]{1,0:T(8,128)S(1)} %get-tuple-element.23.refs_0_), channel_id=1, source_target_pairs={{0,2},{1,3},{2,0},{3,1},{4,6},{5,7},{6,4},{7,5},{8,10},{9,11},{10,... | collective-permute-start | bytes 12296 | tf_op jit(solution)/shard_map/ppermute | solution.py:363
  20.4 4.0 %collective-permute-start.2 = (f32[8,128]{1,0:T(8,128)S(1)}, f32[8,128]{1,0:T(8,128)S(1)}, u32[]{:S(2)}, u32[]{:S(2)}) collective-permute-start(f32[8,128]{1,0:T(8,128)S(1)} %get-tuple-element.23.refs_0_), channel_id=1, source_target_pairs={{0,1},{1,2},{2,3},{3,0},{4,5},{5,6},{6,7},{7,4},{8,9},{9,10},{10,1... | collective-permute-start | bytes 12296 | tf_op jit(solution)/shard_map/ppermute | solution.py:363
  25.1 17.0 %all-to-all-start = ((f32[32,1,1152]{2,1,0:T(1,128)}), f32[32,1,1152]{2,1,0:T(1,128)S(1)}, u32[]{:S(2)}, u32[]{:S(2)}) async-start(f32[32,1,1152]{2,1,0:T(1,128)} %bitcast.11), calls=%async_computation | async-start | bytes 294912 | tf_op jit(solution)/shard_map/all_to_all | solution.py:365
